TPU v7x, 32 devices: a whole 2x2x4 slice. The times are simulated.
32 devices in a mesh: gx: 4 (over y, x), gy: 4 (over z), gz: 2 (over core).
Axes of the slice: x: 2, y: 2, z: 4, core: 2. Of those that a mesh axis runs over, the one named last changes fastest.
Arguments:
- residual: float32 [3, 32, 256, 512], P(None, 'gz', 'gx', 'gy'), may hold values from -32 to 32
- edge_diag: float32 [3, 32, 256, 512], P(None, 'gz', 'gx', 'gy'), may hold values from 6.5 to 9
- node_shift: float32 [32, 256, 512], P('gz', 'gx', 'gy'), may hold values from 0.05 to 3
- coarse_shift: float32 [16, 128, 256], P('gz', 'gx', 'gy'), may hold values from 0.05 to 3
Outputs:
- correction: float32 [3, 32, 256, 512], P(None, 'gz', 'gx', 'gy')
All inputs are finite; a program needn't handle non-finite values.
Results may differ from a plain program's by a relative error of at most 0.000021.
Values sent between devices are 32-bit elements; how exact they have to be, the bound alone decides.
No kernel may reach another device: no remote copies, remote signals or barrier semaphores. Data moves between devices by JAX's collectives and lax.ppermute only.
A program may use at most 128 MiB of HBM per device.

v0:
```python
import itertools

import jax
import jax.numpy as jnp
from jax import lax
from jax.experimental import pallas as pl
from jax.experimental.pallas import tpu as pltpu
from jax.sharding import PartitionSpec as P


F32 = jnp.float32
LANES = 128


def lane_ids(rows):
    return lax.broadcasted_iota(jnp.int32, (rows, LANES), 1)


def row_ids(rows):
    return lax.broadcasted_iota(jnp.int32, (rows, LANES), 0)


def shift_lanes(value, amount):
    return pltpu.roll(value, amount % LANES, 1)


def shift_rows(value, amount):
    return pltpu.roll(value, amount % value.shape[0], 0)


def low_of(axis, size, first, second):
    place = lax.axis_index(axis)
    odd = place % 2 == 1
    zero = jnp.zeros_like(first)
    if second is None:
        return jnp.where(odd, first, zero)
    return jnp.where(odd, first, jnp.where(place > 0, second, zero))


def high_of(axis, size, first, second):
    place = lax.axis_index(axis)
    even = place % 2 == 0
    zero = jnp.zeros_like(first)
    if second is None:
        return jnp.where(even, first, zero)
    return jnp.where(even, first, jnp.where(place < size - 1, second, zero))


def from_below(axis, value):
    return jnp.where(lax.axis_index(axis) > 0, value, jnp.zeros_like(value))


def from_above(axis, size, value):
    return jnp.where(lax.axis_index(axis) < size - 1, value, jnp.zeros_like(value))


def ring(value, axis, step):
    size = lax.axis_size(axis)
    return lax.ppermute(value, axis, [(i, (i + step) % size) for i in range(size)])


def swap(values, axis, names=None):
    size = lax.axis_size(axis)
    out = [lax.ppermute(values[0], axis, [(i, i ^ 1) for i in range(size)])]
    if len(values) == 1:
        return out
    odd = [(i + 1) % size if i % 2 else (i - 1) % size for i in range(size)]
    if names is None:
        out.append(lax.ppermute(values[1], axis, list(enumerate(odd))))
        return out
    main = names.index(axis)
    pairs = []
    sizes = [lax.axis_size(name) for name in names]
    for at in itertools.product(*(range(n) for n in sizes)):
        to = list(at)
        if at[main] in (0, size - 1):
            to[1 - main] ^= 1
        else:
            to[main] = odd[at[main]]
        pairs.append(tuple(p[0] * sizes[1] + p[1] for p in (at, to)))
    out.append(lax.ppermute(values[1], names, pairs))
    return out


def write_sides(axis, refs, up, down):
    even = lax.axis_index(axis) % 2 == 0

    @pl.when(even)
    def _():
        up(refs[0])
        if len(refs) > 1:
            down(refs[1])

    @pl.when(jnp.logical_not(even))
    def _():
        down(refs[0])
        if len(refs) > 1:
            up(refs[1])


def call(body, outs, scratch=(), far=(), far_out=False, **kwargs):
    kind = jax.ShapeDtypeStruct if far_out else pltpu.VMEM
    run = pl.pallas_call(
        body,
        out_shape=[kind(shape, F32) for shape in outs],
        scratch_shapes=[pltpu.VMEM(s, F32) if isinstance(s, tuple) else s for s in scratch],
        compiler_params=pltpu.CompilerParams(vmem_limit_bytes=12 * 2**20),
        **kwargs,
    )

    def apply(*args):
        spaces = [pltpu.HBM if i in far else pltpu.VMEM for i in range(len(args))]
        return run(
            *(
                pltpu.with_memory_space_constraint(a, space)
                for a, space in zip(args, spaces)
            )
        )

    return apply


def vmem(count):
    return [pl.BlockSpec(memory_space=pltpu.VMEM)] * count


def edge_stage(residual, edge_diag):
    _, nz, nx, ny = residual.shape
    step = 4
    steps = nz // step

    def body(res, diag, part, up_z, up_x, up_y, low_z, low_x, low_y, scaled, inv, near, sems):
        lane = lane_ids(nx)
        row = row_ids(nx)

        def copies(block):
            at = pl.ds(block * step, step)
            return [
                pltpu.make_async_copy(source.at[:, at], target.at[:, at], sems.at[i, block])
                for i, (source, target) in enumerate(((res, near), (diag, inv)))
            ]

        for block in range(steps):
            for copy in copies(block):
                copy.start()
        before = jnp.zeros((nx, ny), F32)
        high = jnp.zeros((nx, LANES), F32)
        low = jnp.zeros((nx, LANES), F32)
        for z in range(nz):
            if z % step == 0:
                for copy in copies(z // step):
                    copy.wait()
            s = []
            for k in range(3):
                inverse = 1.0 / inv[k, z]
                inv[k, z] = inverse
                s.append(near[k, z] * inverse)
                scaled[k, z] = s[k]
            total = before - s[0]
            total += jnp.where(row == 0, 0.0, shift_rows(s[1], 1)) - s[1]
            total += jnp.where(lane == 0, 0.0, shift_lanes(s[2], 1)) - s[2]
            part[z] = total
            before = s[0]
            for k in range(3):
                spot = k * nz + z
                up_x[spot : spot + 1, :] = s[k][nx - 1 :, :]
                low_x[spot : spot + 1, :] = s[k][:1, :]
                high = jnp.where(lane == spot, shift_lanes(s[k], spot + 1), high)
                low = jnp.where(lane == spot, shift_lanes(s[k], spot), low)
                if z == 0:
                    low_z[k] = s[k]
                if z == nz - 1:
                    up_z[k] = s[k]
        up_y[...] = high
        low_y[...] = low

    faces = [(3, nx, ny), (3 * nz, ny), (nx, LANES)] * 2
    return call(
        body,
        [(nz, nx, ny)] + faces + [residual.shape] * 2,
        scratch=[residual.shape, pltpu.SemaphoreType.DMA((2, steps))],
        far=(0, 1),
        in_specs=[pl.BlockSpec(memory_space=pltpu.HBM)] * 2,
        out_specs=vmem(9),
    )(residual, edge_diag)


def select_sum(values, chosen):
    first = values.astype(jnp.bfloat16)
    left = values - first.astype(F32)
    second = left.astype(jnp.bfloat16)
    third = (left - second.astype(F32)).astype(jnp.bfloat16)
    chosen = chosen.astype(jnp.bfloat16)
    both = jnp.concatenate([first, second], axis=1)
    total = jnp.dot(both, jnp.concatenate([chosen, chosen], axis=0), preferred_element_type=F32)
    return total + jnp.dot(third, chosen, preferred_element_type=F32)


def plane(values, row_count):
    return jnp.concatenate([values, jnp.zeros((row_count - values.shape[0], LANES), F32)], axis=0)


def nodal_stage(part, node_shift, coarse_shift, got_z, got_x, got_y, z_count):
    nz, nx, ny = part.shape
    cz, cx, cy = nz // 2, nx // 2, ny // 2
    rows = cx + 8
    sends = 1 if z_count == 2 else 2

    def body(part, shift, coarse, gz, gx, gy, fg, rhs, xb, yb, w, *rest):
        out, (pair, stack, s_, xl_, yl_, zl_, zh_) = rest[:sends], rest[sends:]
        lane = lane_ids(nx)
        row = row_ids(nx)
        lane_c = lane_ids(rows)
        row_c = row_ids(rows)
        below_z = from_below("gz", gz[0])
        below_y = from_below("gy", gy[...])
        fine = lax.broadcasted_iota(jnp.int32, (ny, 2 * LANES), 0)
        coarse_lane = lax.broadcasted_iota(jnp.int32, (ny, 2 * LANES), 1)
        miss = jnp.where(
            coarse_lane < LANES, fine // 2 - coarse_lane, fine - 2 * (coarse_lane - LANES)
        )
        gather = jnp.where(miss == 0, 1.0, 0.0)
        for c in range(cz):
            both = []
            for z in (2 * c, 2 * c + 1):
                total = part[z]
                if z == 0:
                    total += below_z
                total += jnp.where(row == 0, from_below("gx", gx[nz + z : nz + z + 1, :]), 0.0)
                total += jnp.where(lane == 0, shift_lanes(below_y, -(2 * nz + z)), 0.0)
                guess = total / (6.0 + shift[z])
                fg[z] = guess
                both.append(guess)
            pair[c % 2] = both[0] + both[1]
            low = pair[c % 2, pl.ds(0, cx, 2), :]
            high = pair[c % 2, pl.ds(1, cx, 2), :]
            first = fg[2 * c, pl.ds(0, cx, 2), :] + fg[2 * c, pl.ds(1, cx, 2), :]
            stack[c, :cx, :] = low + high
            stack[c, cx : 2 * cx, :] = low
            stack[c, 2 * cx :, :] = first
        every = select_sum(stack[...].reshape(3 * cx * cz, LANES), gather)
        for c in range(cz):
            sums = every[3 * cx * c : 3 * cx * (c + 1)]
            s = sums[:cx, :LANES]
            z_low = sums[2 * cx :, :LANES]
            s_[c] = plane(s, rows)
            yl_[c] = plane(sums[:cx, LANES:], rows)
            xl_[c] = plane(sums[cx : 2 * cx, :LANES], rows)
            zl_[c] = plane(z_low, rows)
            zh_[c] = plane(s - z_low, rows)
            w[c] = jnp.zeros((rows, LANES), F32)
            w[c, :cx, :cy] = 1.0 / (6.0 + coarse[c])
        for c in range(cz):
            s, x_low, y_low = s_[c], xl_[c], yl_[c]
            x_high = s - x_low
            y_high = s - y_low
            total = 3.0 * s
            total += shift_rows(x_low, -1) + shift_rows(x_high, 1)
            total += shift_lanes(y_low, -1) + shift_lanes(y_high, 1)
            if c > 0:
                total += zh_[c - 1]
            if c < cz - 1:
                total += zl_[c + 1]
            rhs[c] = total
            xb[c] = jnp.where(row_c < cx // 2, x_low, x_high)
            yb[c] = jnp.where(lane_c < cy // 2, y_low, y_high)
        rhs[cz] = zh_[cz - 1]
        rhs[cz + 1] = jnp.zeros((rows, LANES), F32)
        rhs[cz + 2] = jnp.zeros((rows, LANES), F32)
        rhs[cz + 3] = zl_[0]

        def fill(ref, near, far, half, face):
            planes = [rhs[near], rhs[far], w[near], w[far], half]
            planes += [xb[near], xb[far], yb[near], yb[far]]
            for i, value in enumerate(planes):
                ref[i * rows : (i + 1) * rows, :] = value
            ref[9 * rows : 9 * rows + nx, :] = face

        def up(ref):
            fill(ref, cz - 1, cz - 2, zh_[cz - 1], fg[nz - 1])

        def down(ref):
            fill(ref, 0, 1, zl_[0], fg[0])

        write_sides("gz", out, up, down)

    coarse = (cz, rows, LANES)
    send = (9 * rows + nx, LANES)
    return call(
        body,
        [(nz, nx, ny), (cz + 4, rows, LANES), coarse, coarse, coarse] + [send] * sends,
        scratch=[(2, nx, ny), (cz, 3 * cx, LANES), coarse, coarse, coarse, coarse, coarse],
        in_specs=vmem(6),
        out_specs=vmem(5 + sends),
    )(part, node_shift, coarse_shift, got_z, got_x, got_y)


def x_stage(got, rhs, xb, yb, w, fg, after, z_count, x_count):
    planes, rows, _ = rhs.shape
    cz, cx = planes - 4, rows - 8
    nz, nx, ny = fg.shape
    cy = ny // 2
    sends = 1 if x_count == 2 else 2
    gots = len(got)
    size = -(-(3 * planes + nz + 1) // 8) * 8

    def body(*refs):
        got = refs[:gots]
        rhs, xb, yb, w, fg, _, _, rhs2, w2 = refs[gots : gots + 9]
        out, (xb2, yb2) = refs[gots + 9 : gots + 9 + sends], refs[gots + 9 + sends :]

        def take_at(pick, at):
            values = [ref[at, :] for ref in got]
            return pick("gz", z_count, values[0], values[1] if gots > 1 else None)

        def take(pick, i):
            return take_at(pick, slice(i * rows, (i + 1) * rows))

        for c in range(1, cz - 1):
            rhs2[c] = rhs[c]
        rhs2[0] = rhs[0] + take(low_of, 4)
        rhs2[cz - 1] = rhs[cz - 1] + take(high_of, 4)
        rhs2[cz] = rhs[cz] + take(high_of, 0)
        rhs2[cz + 1] = take(high_of, 1)
        rhs2[cz + 2] = take(low_of, 1)
        rhs2[cz + 3] = rhs[cz + 3] + take(low_of, 0)
        for here, there, i in ((w, w2, 2), (xb, xb2, 5), (yb, yb2, 7)):
            for c in range(cz):
                there[c] = here[c]
            there[cz] = take(high_of, i)
            there[cz + 1] = take(high_of, i + 1)
            there[cz + 2] = take(low_of, i + 1)
            there[cz + 3] = take(low_of, i)

        lane = lane_ids(planes)

        def fill(ref, near, far, fine):
            halves = lane < cy
            first = jnp.where(halves, rhs2[:, near, :], shift_lanes(rhs2[:, far, :], cy))
            second = jnp.where(halves, w2[:, near, :], shift_lanes(w2[:, far, :], cy))
            edge = yb2[:, far, :]
            third = jnp.where(halves, xb2[:, near, :], shift_lanes(yb2[:, near, :], cy))
            third = jnp.where(lane == cy + 1, shift_lanes(edge, cy + 1), third)
            third = jnp.where(lane == LANES - 2, shift_lanes(edge, cy - 1), third)
            for i, value in enumerate((first, second, third)):
                ref[i * planes : (i + 1) * planes, :] = value
            ref[3 * planes : 3 * planes + nz, :] = fg[:, fine, :]
            at = 9 * rows + fine
            last = 3 * planes + nz
            ref[last : last + 1, :] = take_at(high_of, slice(at, at + 1))
            ref[last + 1 :, :] = jnp.zeros((size - last - 1, LANES), F32)

        def up(ref):
            fill(ref, cx - 1, cx - 2, nx - 1)

        def down(ref):
            fill(ref, 0, 1, 0)

        write_sides("gx", out, up, down)

    whole = (planes, rows, LANES)
    return call(
        body,
        [whole, whole] + [(size, LANES)] * sends,
        scratch=[whole, whole],
        in_specs=vmem(gots + 7),
        out_specs=vmem(2 + sends),
    )(*got, rhs, xb, yb, w, fg, *after)


def x_tail(got, fg, node_shift, low_x, after, z_count):
    nz, nx, ny = fg.shape
    z_at = 9 * (nx // 2 + 8)
    gots = len(got)

    def body(*refs):
        got = refs[:gots]
        fg, shift, low_x, _, out = refs[gots:]
        lane = lane_ids(nz)
        row = row_ids(nz)

        def z_row(pick):
            values = [ref[z_at : z_at + 1, :] for ref in got]
            return pick("gz", z_count, values[0], values[1] if gots > 1 else None)

        here = fg[:, 0, :]
        around = fg[:, 1, :] + jnp.where(row == 0, z_row(low_of), shift_rows(here, 1))
        around += jnp.where(row == nz - 1, z_row(high_of), shift_rows(here, -1))
        around += jnp.where(lane == 0, 0.0, shift_lanes(here, 1))
        around += jnp.where(lane == ny - 1, 0.0, shift_lanes(here, -1))
        inverse = 1.0 / (6.0 + shift[:, 0, :])
        out[: 3 * nz, :] = low_x[...]
        out[3 * nz : 4 * nz, :] = here + inverse * around
        out[4 * nz :, :] = inverse

    return call(
        body, [(5 * nz, LANES)], in_specs=vmem(gots + 4), out_specs=vmem(1)
    )(*got, fg, node_shift, low_x, after)[0]


def part_stage(fg, node_shift, low_z):
    nz, nx, ny = fg.shape

    def body(fg, shift, low_z, part, inv, tail):
        lane = lane_ids(nx)
        row = row_ids(nx)
        zero = jnp.zeros((nx, ny), F32)
        for z in range(nz):
            guess = fg[z]
            inner = fg[z + 1] if z < nz - 1 else zero
            inner += jnp.where(row == 0, 0.0, shift_rows(guess, 1))
            inner += jnp.where(row == nx - 1, 0.0, shift_rows(guess, -1))
            inner += jnp.where(lane == 0, 0.0, shift_lanes(guess, 1))
            inner += jnp.where(lane == ny - 1, 0.0, shift_lanes(guess, -1))
            inverse = 1.0 / (6.0 + shift[z])
            inv[z] = inverse
            part[z] = guess + inverse * (inner + (fg[z - 1] if z > 0 else zero))
            if z == 0:
                for k in range(3):
                    tail[k * nx : (k + 1) * nx, :] = low_z[k]
                tail[3 * nx : 4 * nx, :] = guess + inverse * inner
                tail[4 * nx :, :] = inverse

    return call(
        body, [fg.shape, fg.shape, (5 * nx, LANES)], in_specs=vmem(3), out_specs=vmem(3)
    )(fg, node_shift, low_z)


def fold_row(rows):
    return (rows + 8) // 16 * 8


def line(source, lane, fine, at):
    acc = jnp.zeros(lane.shape, F32)
    for z in range(source.shape[0]):
        moved = jnp.broadcast_to(source[z : z + 1, :], lane.shape)
        acc = jnp.where(lane == at + z, shift_lanes(moved, at + z - fine), acc)
    return acc


def y_stage(got, rhs, w, early, x_count, y_count):
    planes, rows, _ = rhs.shape
    cx = rows - 8
    nx, cy = 2 * cx, LANES // 2
    nz, half, cut = 2 * (planes - 4), nx // 2, fold_row(rows)
    sends = 1 if y_count == 2 else 2
    gots = len(got)

    def body(*refs):
        got = refs[:gots]
        rhs, w, up_, down_, part, inv, _, rhs3, w3 = refs[gots : gots + 9]
        rest = refs[gots + 9 :]
        out, (add,) = rest[:sends], rest[sends:]
        lane_p = lane_ids(planes)

        def take_at(pick, at):
            values = [ref[at, :] for ref in got]
            return pick("gx", x_count, values[0], values[1] if gots > 1 else None)

        def take(pick, i):
            return take_at(pick, slice(i * planes, (i + 1) * planes))

        add[...] = jnp.zeros_like(add)
        for c in range(planes):
            w3[c] = w[c]
        for pick, near, far, edge in ((high_of, cx, cx + 1, cx - 1), (low_of, rows - 1, rows - 2, 0)):
            first, second, third = take(pick, 0), take(pick, 1), take(pick, 2)
            other = shift_lanes(third, -cy)
            one = jnp.where((lane_p == 0) | (lane_p == cy - 1), other, 0.0)
            two = jnp.where(lane_p == 0, shift_lanes(third, -cy - 1), 0.0)
            two = jnp.where(lane_p == cy - 1, shift_lanes(third, 1 - cy), two)
            for at, value, ends in ((near, first, one), (far, shift_lanes(first, -cy), two)):
                value = jnp.where(lane_p < cy, value, 0.0)
                value += jnp.where(lane_p == cy, shift_lanes(ends, 1), 0.0)
                value += jnp.where(lane_p == LANES - 1, shift_lanes(ends, -1), 0.0)
                add[:, at, :] = value
            w3[:, near, :] = jnp.where(lane_p < cy, second, 0.0)
            w3[:, far, :] = jnp.where(lane_p < cy, shift_lanes(second, -cy), 0.0)
            add[:, edge, :] = jnp.where(lane_p < cy, third, 0.0)
        for c in range(planes):
            rhs3[c] = rhs[c] + add[c]

        lane_c = lane_ids(rows)
        lane8 = lane_ids(8)
        base = 5 * planes
        x_face = slice(3 * planes, 3 * planes + nz)
        x_high = take_at(high_of, x_face)

        def fill(ref, first, fine, early):
            acc = jnp.zeros((rows, LANES), F32)
            inner = first if first > 0 else 0
            for z in range(planes):
                for field, width, at, source in (
                    (rhs3, 3, 3 * z, first),
                    (w3, 2, 3 * planes + 2 * z, inner),
                ):
                    there = (lane_c >= at) & (lane_c < at + width)
                    acc = jnp.where(there, shift_lanes(field[z], at - source), acc)
            ref[:cut, :] = acc[:cut]
            ref[: rows - cut, :] += shift_lanes(acc[cut:], base)
            ref[cut - 8 : cut, :] += line(x_high, lane8, fine, base)
            ref[cut:, :] = early

        def up(ref):
            fill(ref, cy - 2, 2 * cy - 1, up_[...])

        def down(ref):
            row = row_ids(nx)
            ends = jnp.where(row == 0, line(take_at(low_of, x_face), lane8, 0, 0)[:1, :], 0.0)
            ends += jnp.where(row == nx - 1, line(x_high, lane8, 0, 0)[:1, :], 0.0)
            inverse = inv[...]
            value = part[...] + inverse * ends
            packed = down_[...]
            for i, source in (
                (1, value[:half]),
                (2, inverse[:half]),
                (4, value[half:]),
                (5, inverse[half:]),
            ):
                there = lane_ids(half) // nz == i
                packed = jnp.where(there, shift_lanes(source, i * nz), packed)
            fill(ref, -1, 0, packed)

        write_sides("gy", out, up, down)

    whole = (planes, rows, LANES)
    return call(
        body,
        [whole, whole] + [(cut + half, LANES)] * sends,
        scratch=[whole],
        in_specs=vmem(gots + 7),
        out_specs=vmem(2 + sends),
    )(*got, rhs, w, *early)


def y_columns(fg, node_shift):
    nz, nx, _ = fg.shape

    def body(fg, shift, here_, inner_, high_, inv):
        lane = lane_ids(nx)
        zero = jnp.zeros((nx, LANES), F32)
        here, inner, high, inverse = zero, zero, zero, zero + 1.0
        for z in range(nz):
            guess = fg[z]
            here = jnp.where(lane == z, shift_lanes(guess, z), here)
            inner = jnp.where(lane == z, shift_lanes(guess, z - 1), inner)
            high = jnp.where(lane == z, shift_lanes(guess, z + 1), high)
            inverse = jnp.where(lane == z, shift_lanes(6.0 + shift[z], z), inverse)
        here_[...] = here
        inner_[...] = inner
        high_[...] = high
        inv[...] = 1.0 / inverse

    return call(body, [(nx, LANES)] * 4, in_specs=vmem(2), out_specs=vmem(4))(fg, node_shift)


def y_early(got_z, columns, after, nz, z_count):
    nx = columns[0].shape[0]
    z_at = 9 * (nx // 2 + 8)
    n_z = len(got_z)

    def body(*refs):
        gz = refs[:n_z]
        here_, inner, high_, inv, _, up, down, part, last = refs[n_z:]
        lane = lane_ids(nx)
        row = row_ids(nx)

        def side(pick):
            values = [ref[z_at : z_at + nx, :] for ref in gz]
            return pick("gz", z_count, values[0], values[1] if n_z > 1 else None)

        above = side(high_of)
        here = jnp.where(lane == nz, shift_lanes(above, nz), here_[...])
        here = jnp.where(lane == LANES - 1, shift_lanes(side(low_of), -1), here)
        high = jnp.where(lane == nz, shift_lanes(above, nz + 1), high_[...])
        inverse = inv[...]
        around = inner[...] + shift_lanes(here, 1) + shift_lanes(here, -1)
        around += jnp.where(row == 0, 0.0, shift_rows(here, 1))
        around += jnp.where(row == nx - 1, 0.0, shift_rows(here, -1))
        last[...] = high
        half = nx // 2
        lane_h = lane_ids(half)

        def fold(value):
            first, second = value[:half], value[half:]
            block = jnp.where(lane_h < nz, first, 0.0)
            there = (lane_h >= 3 * nz) & (lane_h < 4 * nz)
            block = jnp.where(there, shift_lanes(second, 3 * nz), block)
            block = jnp.where(lane_h == 6 * nz, shift_lanes(first, 5 * nz), block)
            return jnp.where(lane_h == 6 * nz + 1, shift_lanes(second, 5 * nz + 1), block)

        up[...] = fold(high)
        down[...] = fold(here)
        part[...] = here + inverse * around

    return call(
        body, [(nx // 2, LANES)] * 2 + [(nx, LANES)] * 2, in_specs=vmem(n_z + 5), out_specs=vmem(4)
    )(*got_z, *columns, after)


def coarse_stage(got, rhs, w, after, y_count, devices):
    planes, rows, _ = rhs.shape
    cz, cx = planes - 4, rows - 8
    cy = LANES // 2
    gots = len(got)

    def body(*refs):
        got = refs[:gots]
        rhs, w, _, v1, v2, sums, tot, inv_, image_ = refs[gots:]
        cut = fold_row(rows)
        tail = [shift_lanes(ref[: rows - cut, :], -5 * planes) for ref in got]
        values = [jnp.concatenate([ref[:cut, :], t], axis=0) for ref, t in zip(got, tail)]
        second = values[1] if gots > 1 else None
        low = low_of("gy", y_count, values[0], second)
        high = high_of("gy", y_count, values[0], second)
        lane = lane_ids(rows)
        above = (lane >= cy - 1) & (lane < cy + 2)
        below = (lane >= LANES - 2) | (lane == 0)
        for z in range(planes):
            at = 3 * z
            right = jnp.where(below, shift_lanes(low, LANES - 2 - at), 0.0)
            right = rhs[z] + jnp.where(above, shift_lanes(high, cy - 1 - at), right)
            at = 3 * planes + 2 * z
            inv = jnp.where(lane >= LANES - 2, shift_lanes(low, LANES - 2 - at), w[z])
            inv = jnp.where((lane >= cy) & (lane < cy + 2), shift_lanes(high, cy - at), inv)
            inv_[z] = inv
            tot[z] = right
            v1[z] = right * inv

        def near(field, z):
            here = field[z]
            total = field[(z + 1) % planes] + field[(z - 1) % planes]
            total += shift_rows(here, 1) + shift_rows(here, -1)
            return total + shift_lanes(here, 1) + shift_lanes(here, -1)

        v2[cz + 1] = jnp.zeros((rows, LANES), F32)
        v2[cz + 2] = jnp.zeros((rows, LANES), F32)
        for z in list(range(cz + 1)) + [planes - 1]:
            image = tot[z] - near(v1, z)
            if z < cz:
                image_[z] = image
            v2[z] = image * inv_[z]
        parts = [jnp.zeros((cx, LANES), F32)] * 5
        for z in range(cz):
            first, second_, right, image = v1[z], v2[z], tot[z], image_[z]
            third = image - near(v2, z)
            terms = (first * right, second_ * right, first * image, second_ * image, second_ * third)
            parts = [a + b[:cx, :] for a, b in zip(parts, terms)]
        keep = lane_ids(1) < cy
        lines = [jnp.where(keep, jnp.sum(a, axis=0, keepdims=True), 0.0) for a in parts]
        tile = jnp.concatenate(lines + [jnp.zeros((3, LANES), F32)], axis=0)
        column = jnp.sum(tile, axis=1, keepdims=True)
        spread = jnp.where(lane_ids(8) == row_ids(8), column, 0.0)
        line = jnp.sum(spread, axis=0, keepdims=True)
        sums[...] = jnp.broadcast_to(line[None], (devices, 1, LANES))

    whole = (planes, rows, LANES)
    return call(
        body,
        [whole, whole, (devices, 1, LANES)],
        scratch=[whole, whole, whole],
        in_specs=vmem(gots + 3),
        out_specs=vmem(3),
    )(*got, rhs, w, *after)


def smooth_stage(scaled, inverses, below, tail_z, tail_x, tail_y, after, counts):
    _, nz, nx, _ = scaled.shape

    def body(*refs):
        s, inv, lz, lx, ly = refs[:5]
        tz, gx, ty, _, out = refs[5:]
        lane = lane_ids(nx)
        row = row_ids(nx)
        y_low = from_below("gy", ly[...])

        y_high = from_above("gy", counts[2], ty[...])
        for k in range(3):
            z_low = from_below("gz", lz[k])
            z_high = from_above("gz", counts[0], tz[k * nx : (k + 1) * nx, :])
            x_low = from_below("gx", lx[k * nz : (k + 1) * nz, :])
            x_high = from_above("gx", counts[1], gx[k * nz : (k + 1) * nz, :])
            for z in range(nz):
                here = s[k, z]
                around = s[k, z - 1] if z > 0 else z_low
                around += s[k, z + 1] if z < nz - 1 else z_high
                around += jnp.where(row == 0, x_low[z : z + 1, :], shift_rows(here, 1))
                around += jnp.where(row == nx - 1, x_high[z : z + 1, :], shift_rows(here, -1))
                spot = k * nz + z
                around += jnp.where(lane == 0, shift_lanes(y_low, -spot), shift_lanes(here, 1))
                right = shift_lanes(y_high, -spot - 1)
                around += jnp.where(lane == LANES - 1, right, shift_lanes(here, -1))
                out[k, z] = here + around * inv[k, z]

    return call(
        body, [scaled.shape], in_specs=vmem(9), out_specs=vmem(1)
    )(scaled, inverses, *below, tail_z, tail_x, tail_y, after)[0]


def final_stage(sums, v1, v2, fg, mid, smooth, early, tail_z, tail_x, got_z, got_x, got_y, counts):
    planes, rows, _ = v1.shape
    cz, cx, cy = planes - 4, rows - 8, LANES // 2
    nz, nx, _ = fg.shape
    step = 2
    n_z, n_x, n_y = len(got_z), len(got_x), len(got_y)
    gots = n_z + n_x + n_y

    def body(*refs):
        sums, v1, v2, fg, part, inv, smooth, early, tz, tx = refs[:10]
        gz = refs[10 : 10 + n_z]
        gx = refs[10 + n_z : 10 + n_z + n_x]
        gy = refs[10 + n_z + n_x : 10 + gots]
        out, sol, dup, inter, small, lines, buf, sem = refs[10 + gots :]

        def one_side(pick, refs, axis, size, at):
            values = [ref[at, :] for ref in refs]
            return pick(axis, size, values[0], values[1] if len(values) > 1 else None)

        def both(refs, axis, size, at):
            return [one_side(pick, refs, axis, size, at) for pick in (low_of, high_of)]

        total = jnp.sum(sums[...], axis=0)
        lane1 = lane_ids(1)
        gone, gtwo, hone, hmix, htwo = [
            jnp.sum(jnp.where(lane1 == i, total, 0.0), axis=1, keepdims=True) for i in range(5)
        ]
        two = (gtwo - hmix * gone / hone) / (htwo - hmix * hmix / hone)
        one = (gone - hmix * two) / hone
        source = lax.broadcasted_iota(jnp.int32, (LANES, 2 * LANES), 0)
        target = lax.broadcasted_iota(jnp.int32, (LANES, 2 * LANES), 1)
        fine = target - LANES
        side = jnp.where(fine % 2 == 1, fine // 2 + 1, (fine // 2 + LANES - 1) % LANES)
        spread = jnp.where(jnp.where(target < LANES, target // 2, side) == source, 1.0, 0.0)
        for z in range(planes):
            sol[z] = one * v1[z] + two * v2[z]
        every = select_sum(sol[...].reshape(planes * rows, LANES), spread)
        dup[...] = every.reshape(planes, rows, 2 * LANES)

        z_low, z_high = both(gz, "gz", counts[0], slice(9 * rows, 9 * rows + nx))
        x_low, x_high = both(gx, "gx", counts[1], slice(3 * planes, 3 * planes + nz + 1))
        half, cut = nx // 2, fold_row(rows)
        y_row_low, y_row_high = both(gy, "gy", counts[2], slice(cut - 8, cut - 7))
        y_packs = both(gy, "gy", counts[2], slice(cut, cut + half))
        lane_h = lane_ids(half)

        def unfold(pack):
            first = jnp.where(lane_h < nz, pack, shift_lanes(pack, -5 * nz))
            second = shift_lanes(pack, -5 * nz - 1)
            second = jnp.where(lane_h < nz, shift_lanes(pack, -3 * nz), second)
            return jnp.concatenate([first, second], axis=0)

        y_low, y_high = [unfold(pack) for pack in y_packs]
        y_pack = y_packs[1]
        lane = lane_ids(nx)
        row = row_ids(nx)
        base = 5 * planes

        def spread_around(z):
            c, odd = z // 2, z % 2
            here = dup[c, :, :LANES]
            same = 3.0 * here + dup[c, :, LANES:]
            same += dup[(c + 1 if odd else c - 1) % planes, :, :LANES]
            slot = z % 2
            inter[slot, pl.ds(0, cx, 2), :] = (same + shift_rows(here, 1))[:cx, :]
            inter[slot, pl.ds(1, cx, 2), :] = (same + shift_rows(here, -1))[:cx, :]
            return inter[slot]

        def nodal(z):
            around = spread_around(z) + jnp.where(row == 0, x_low[z : z + 1, :], 0.0)
            around += jnp.where(row == nx - 1, x_high[z : z + 1, :], 0.0)
            around += jnp.where(lane == 0, shift_lanes(y_low, -z), 0.0)
            around += jnp.where(lane == LANES - 1, shift_lanes(y_high, -z - 1), 0.0)
            if z == nz:
                value = tz[3 * nx : 4 * nx, :] + tz[4 * nx :, :] * (around + fg[nz - 1])
                return from_above("gz", counts[0], value)
            if z == 0:
                around += z_low
            if z == nz - 1:
                around += z_high
            return part[z] + inv[z] * around

        here = dup[:cz, cx, :LANES]
        same = 3.0 * here + dup[:cz, cx, LANES:] + dup[:cz, cx - 1, :LANES]
        small[pl.ds(0, cz, 2), :] = same + jnp.concatenate(
            [dup[planes - 1, cx : cx + 1, :LANES], here[: cz - 1]], axis=0
        )
        small[pl.ds(1, cz, 2), :] = same + dup[1 : cz + 1, cx, :LANES]
        for z in range(nz):
            left = shift_lanes(y_row_low, -(base + z))
            right = shift_lanes(y_row_high, -(base + z) - 1)
            value = jnp.where(lane1 == 0, left, 0.0)
            lines[z : z + 1, :] = jnp.where(lane1 == LANES - 1, right, value)
        x_value = tx[3 * nz : 4 * nz, :] + tx[4 * nz :, :] * (
            fg[:, nx - 1, :] + small[...] + lines[...]
        )
        x_value = from_above("gx", counts[1], x_value)

        lane_c = lane_ids(rows)
        even = jnp.zeros((rows, LANES), F32)
        odd = jnp.zeros((rows, LANES), F32)
        for z in range(nz):
            c = z // 2
            here = sol[c]
            same = 3.0 * here + shift_lanes(here, 1) + sol[(c + 1 if z % 2 else c - 1) % planes]
            even = jnp.where(lane_c == z, shift_lanes(same + shift_rows(here, 1), z - cy), even)
            odd = jnp.where(lane_c == z, shift_lanes(same + shift_rows(here, -1), z - cy), odd)
        inter[0, pl.ds(0, cx, 2), :] = even[:cx, :]
        inter[0, pl.ds(1, cx, 2), :] = odd[:cx, :]
        y_base = jnp.concatenate(
            [shift_lanes(y_pack, -nz), shift_lanes(y_pack, -4 * nz)], axis=0
        )
        y_inverse = jnp.concatenate(
            [shift_lanes(y_pack, -2 * nz), shift_lanes(y_pack, -5 * nz)], axis=0
        )
        y_value = y_base + y_inverse * (early[...] + inter[0])
        y_value = from_above("gy", counts[2], y_value)

        def copy(block):
            at = pl.ds(block * step, step)
            return pltpu.make_async_copy(buf.at[:, at], out.at[:, at], sem.at[block])

        value = nodal(0)
        for z in range(nz):
            after = nodal(z + 1)
            steps = [after, jnp.where(row == nx - 1, x_value[z : z + 1, :], shift_rows(value, -1))]
            steps.append(
                jnp.where(lane == LANES - 1, shift_lanes(y_value, -z - 1), shift_lanes(value, -1))
            )
            for k in range(3):
                buf[k, z] = smooth[k, z] + (steps[k] - value)
            if z % step == step - 1:
                copy(z // step).start()
            value = after
        for block in range(nz // step):
            copy(block).wait()

    return call(
        body,
        [smooth.shape],
        scratch=[
            (planes, rows, LANES),
            (planes, rows, 2 * LANES),
            (2, nx, LANES),
            (nz, LANES),
            (nz, LANES),
            smooth.shape,
            pltpu.SemaphoreType.DMA((nz // step,)),
        ],
        far_out=True,
        in_specs=vmem(10 + gots),
        out_specs=[pl.BlockSpec(memory_space=pltpu.HBM)],
    )(sums, v1, v2, fg, *mid, smooth, early, tail_z, tail_x, *got_z, *got_x, *got_y)[0]


def local(residual, edge_diag, node_shift, coarse_shift):
    axes = ("gz", "gx", "gy")
    counts = tuple(lax.axis_size(a) for a in axes)
    devices = counts[0] * counts[1] * counts[2]
    part, *faces, scaled, inverses = edge_stage(residual, edge_diag)
    up_z, up_x, up_y, low_z, low_x, low_y = faces
    below = []
    for value, axis in ((up_z, "gz"), (up_x, "gx"), (up_y, "gy")):
        below.append(ring(value, axis, 1))
    tail_y = ring(low_y, "gy", -1)
    fg, rhs, xb, yb, w, *send = nodal_stage(part, node_shift, coarse_shift, *below, counts[0])
    got_z = swap(send, "gz")
    *mid, tail_z = part_stage(fg, node_shift, low_z)
    columns = y_columns(fg, node_shift)
    after = (mid[1], columns[0])
    rhs, w, *send = x_stage(got_z, rhs, xb, yb, w, fg, after, counts[0], counts[1])
    got_x = swap(send, "gx", ("gx", "gz"))
    tail_x = x_tail(got_z, fg, node_shift, low_x, w, counts[0])
    *early, last = y_early(got_z, columns, w, fg.shape[0], counts[0])
    early = (*early, columns[3], tail_x)
    tail_z = ring(tail_z, "gz", -1)
    tail_x = ring(tail_x, "gx", -1)
    rhs, w, *send = y_stage(got_x, rhs, w, early, counts[1], counts[2])
    got_y = swap(send, "gy", ("gy", "gz"))
    smooth = smooth_stage(scaled, inverses, below, tail_z, tail_x, tail_y, w, counts)
    v1, v2, sums = coarse_stage(got_y, rhs, w, (smooth,), counts[2], devices)
    sums = lax.all_to_all(sums, ("gx", "gy", "gz"), 0, 0)
    return final_stage(
        sums, v1, v2, fg, mid, smooth, last, tail_z, tail_x, got_z, got_x, got_y, counts
    )


def solution(mesh):
    placed = (
        P(None, "gz", "gx", "gy"),
        P(None, "gz", "gx", "gy"),
        P("gz", "gx", "gy"),
        P("gz", "gx", "gy"),
    )

    return jax.shard_map(
        local, mesh=mesh, in_specs=placed, out_specs=P(None, "gz", "gx", "gy"), check_vma=False
    )
```

profile of v0, /device:TPU:0, one launch (start us, length us, event | category | flops | bytes accessed | tf_op | source)
XLA Modules:
  0.0 37.2 jit_solution(7318078486541645482)
XLA Ops:
  0.0 2.5 %shard_map.46 = (f32[16,64,128]{2,1,0:T(8,128)S(1)}, f32[3,64,128]{2,1,0:T(8,128)S(1)}, f32[48,128]{1,0:T(8,128)S(1)}, f32[64,128]{1,0:T(8,128)S(1)}, f32[3,64,1...) custom-call(f32[3,16,64,128]{3,2,1,0:T(8,128)} %res.1, ...), custom_call_target="tpu_custom_call" | custom-call | tf_op jit(solution)/shard_map/pallas_call | solution.py:113
  2.5 0.6 %collective-permute-start = (f32[3,64,128]{2,1,0:T(8,128)S(1)}, f32[3,64,128]{2,1,0:T(8,128)S(1)}, u32[]{:S(2)}, u32[]{:S(2)}) collective-permute-start(f32[3,64,128]{2,1,0:T(8,128)S(1)} %get-tuple-element.43), channel_id=1, source_target_pairs={{0,1},{1,0},{2,3},{3,2},{4,5},{5,4},{6,7},{7,6},{8,9},{9,8},{10,11... | collective-permute-start | bytes 294920 | tf_op jit(solution)/shard_map/ppermute | solution.py:59
  3.1 2.6 %collective-permute-start.2 = (f32[64,128]{1,0:T(8,128)S(1)}, f32[64,128]{1,0:T(8,128)S(1)}, u32[]{:S(2)}, u32[]{:S(2)}) collective-permute-start(f32[64,128]{1,0:T(8,128)S(1)} %get-tuple-element.45), channel_id=1, source_target_pairs={{0,2},{2,4},{4,6},{6,0},{1,3},{3,5},{5,7},{7,1},{8,10},{10,12},{12... | collective-permute-start | bytes 98312 | tf_op jit(solution)/shard_map/ppermute | solution.py:59
  5.7 1.5 %collective-permute-start.1 = (f32[48,128]{1,0:T(8,128)S(1)}, f32[48,128]{1,0:T(8,128)S(1)}, u32[]{:S(2)}, u32[]{:S(2)}) collective-permute-start(f32[48,128]{1,0:T(8,128)S(1)} %get-tuple-element.44), channel_id=1, source_target_pairs={{0,8},{8,16},{16,24},{24,0},{1,9},{9,17},{17,25},{25,1},{2,10},{10... | collective-permute-start | bytes 73736 | tf_op jit(solution)/shard_map/ppermute | solution.py:59
  7.2 3.2 %collective-permute-done.1.gx.refs_3_ = f32[48,128]{1,0:T(8,128)S(1)} collective-permute-done((f32[48,128]{1,0:T(8,128)S(1)}, f32[48,128]{1,0:T(8,128)S(1)}, u32[]{:S(2)}, u32[]{:S(2)}) %collective-permute-start.1) | collective-permute-done | bytes 24608 | tf_op jit(solution)/shard_map/ppermute | solution.py:59
  10.4 0.5 %shard_map.47 = (f32[16,64,128]{2,1,0:T(8,128)S(1)}, f32[12,40,128]{2,1,0:T(8,128)S(1)}, f32[8,40,128]{2,1,0:T(8,128)S(1)}, f32[8,40,128]{2,1,0:T(8,128)S(1)}, f...) custom-call(f32[16,64,128]{2,1,0:T(8,128)S(1)} %get-tuple-element.42.part, f32[16,64,128]{2,1,0:T(8,128)S(1)} %copy-done, ...), custom_call_target="tpu_custom_call" | custom-call | tf_op jit(solution)/shard_map/pallas_call | solution.py:113
  11.0 0.1 collective-permute-start.3
  11.1 0.4 shard_map.48
  11.4 0.6 %collective-permute-start.8 = (f32[320,128]{1,0:T(8,128)S(1)}, f32[320,128]{1,0:T(8,128)S(1)}, u32[]{:S(2)}, u32[]{:S(2)}) collective-permute-start(f32[320,128]{1,0:T(8,128)S(1)} %get-tuple-element.72), channel_id=1, source_target_pairs={{0,1},{1,0},{2,3},{3,2},{4,5},{5,4},{6,7},{7,6},{8,9},{9,8},{10,11... | collective-permute-start | bytes 491528 | tf_op jit(solution)/shard_map/ppermute | solution.py:59
  12.0 0.6 %shard_map.49 = (f32[64,128]{1,0:T(8,128)S(1)}, f32[64,128]{1,0:T(8,128)S(1)}, f32[64,128]{1,0:T(8,128)S(1)}, f32[64,128]{1,0:T(8,128)S(1)}) custom-call(f32[16,64,128]{2,1,0:T(8,128)S(1)} %get-tuple-element.51.fg.refs_5_.refs_1_.refs_3_, f32[16,64,128]{2,1,0:T(8,128)S(1)} %copy-done), custom_call_target="tpu_custom_call" | custom-call | tf_op jit(solution)/shard_map/pallas_call | solution.py:113
  12.6 0.2 shard_map.50
  12.8 1.0 %collective-permute-start.4 = (f32[56,128]{1,0:T(8,128)S(1)}, f32[56,128]{1,0:T(8,128)S(1)}, u32[]{:S(2)}, u32[]{:S(2)}) collective-permute-start(f32[56,128]{1,0:T(8,128)S(1)} %get-tuple-element.55), channel_id=1, source_target_pairs={{0,8},{8,0},{16,24},{24,16},{1,9},{9,1},{17,25},{25,17},{2,10},{10... | collective-permute-start | bytes 86024 | tf_op jit(solution)/shard_map/ppermute | solution.py:64
  13.7 0.1 shard_map.52.refs_8_
  13.8 2.1 %collective-permute-start.9 = (f32[80,128]{1,0:T(8,128)S(1)}, f32[80,128]{1,0:T(8,128)S(1)}, u32[]{:S(2)}, u32[]{:S(2)}) collective-permute-start(f32[80,128]{1,0:T(8,128)S(1)} %shard_map.52.refs_8_), channel_id=1, source_target_pairs={{0,24},{8,0},{16,8},{24,16},{1,25},{9,1},{17,9},{25,17},{2,26},{10... | collective-permute-start | bytes 122888 | tf_op jit(solution)/shard_map/ppermute | solution.py:59
  15.9 2.2 %collective-permute-start.10 = (f32[64,128]{1,0:T(8,128)S(1)}, f32[64,128]{1,0:T(8,128)S(1)}, u32[]{:S(2)}, u32[]{:S(2)}) collective-permute-start(f32[64,128]{1,0:T(8,128)S(1)} %get-tuple-element.73), channel_id=1, source_target_pairs={{0,6},{2,0},{4,2},{6,4},{1,7},{3,1},{5,3},{7,5},{8,14},{10,8},{12,... | collective-permute-start | bytes 98312 | tf_op jit(solution)/shard_map/ppermute | solution.py:59
  18.2 0.2 shard_map.51
  18.4 0.8 %shard_map.53 = (f32[12,40,128]{2,1,0:T(8,128)S(1)}, f32[12,40,128]{2,1,0:T(8,128)S(1)}, f32[56,128]{1,0:T(8,128)S(1)}, f32[56,128]{1,0:T(8,128)S(1)}) custom-call(f32[56,128]{1,0:T(8,128)S(1)} %collective-permute-done.4.refs_0_.refs_11_, f32[56,128]{1,0:T(8,128)S(1)} %collective-permute-done.5.refs_1_.refs_12_, ...), custom_call_target="tpu_custom_call" | custom-call | tf_op jit(solution)/shard_map/pallas_call | solution.py:113
  19.2 0.1 collective-permute-start.7
  19.3 0.5 %collective-permute-done.10.refs_7_ = f32[64,128]{1,0:T(8,128)S(1)} collective-permute-done((f32[64,128]{1,0:T(8,128)S(1)}, f32[64,128]{1,0:T(8,128)S(1)}, u32[]{:S(2)}, u32[]{:S(2)}) %collective-permute-start.10) | collective-permute-done | bytes 32800 | tf_op jit(solution)/shard_map/ppermute | solution.py:59
  19.8 1.7 %shard_map.54.refs_4_.refs_6_ = f32[3,16,64,128]{3,2,1,0:T(8,128)S(1)} custom-call(f32[3,16,64,128]{3,2,1,0:T(8,128)S(1)} %get-tuple-element.70.refs_0_, f32[3,16,64,128]{3,2,1,0:T(8,128)S(1)} %get-tuple-element.71.refs_1_, f32[3,64,128]{2,1,0:T(8,128)S(1)} %collective-permute-done.gz.refs_2_, f32[48,128]{1,0:T(8,128)S(1)} %collective-permute-done.1.gx.refs_3_, ...), custom_call_target="tpu_custom_call" | custom-call | tf_op jit(solution)/shard_map/pallas_call | solution.py:113
  21.5 1.5 %collective-permute-done.6.refs_0_.refs_13_ = f32[56,128]{1,0:T(8,128)S(1)} collective-permute-done((f32[56,128]{1,0:T(8,128)S(1)}, f32[56,128]{1,0:T(8,128)S(1)}, u32[]{:S(2)}, u32[]{:S(2)}) %collective-permute-start.6) | collective-permute-done | bytes 28704 | tf_op jit(solution)/shard_map/ppermute | solution.py:64
  23.1 0.7 %shard_map.55 = (f32[12,40,128]{2,1,0:T(8,128)S(1)}, f32[12,40,128]{2,1,0:T(8,128)S(1)}, f32[32,1,128]{2,1,0:T(1,128)S(1)}) custom-call(f32[56,128]{1,0:T(8,128)S(1)} %collective-permute-done.6.refs_0_.refs_13_, f32[56,128]{1,0:T(8,128)S(1)} %collective-permute-done.7.refs_1_.refs_14_, f32[12,40,128]{2,1,0:T(8,128)S(1)} %get-tuple-element.68.refs_2_, ...), custom_call_target="tpu_custom_call" | custom-call | tf_op jit(solution)/shard_map/pallas_call | solution.py:113
  23.7 11.4 %all_to_all.5.refs_0_ = f32[32,1,128]{2,1,0:T(1,128)S(1)} all-to-all(f32[32,1,128]{2,1,0:T(1,128)S(1)} %get-tuple-element.74), channel_id=1, replica_groups=mesh['gx'=4,'gy'=4,'gz'=2] {'gx','gy','gz'}, dimensions={0} | all-to-all | bytes 32768 | tf_op jit(solution)/shard_map/all_to_all | solution.py:881
  35.1 2.1 %shard_map.56 = f32[3,16,64,128]{3,2,1,0:T(8,128)} custom-call(f32[32,1,128]{2,1,0:T(1,128)S(1)} %all_to_all.5.refs_0_, f32[12,40,128]{2,1,0:T(8,128)S(1)} %get-tuple-element.75.refs_1_, f32[12,40,128]{2,1,0:T(8,128)S(1)} %get-tuple-element.76.refs_2_, f32[16,64,128]{2,1,0:T(8,128)S(1)} %get-tuple-element.51.fg.refs_5_.refs_1_.refs_3_, ...), custom_call_target="tpu_custom_call" | custom-call | tf_op jit(solution)/shard_map/pallas_call | solution.py:113
  (14 shorter events, 0.1 us)
Async XLA Ops:
  0.0 10.4 %copy-start = (f32[16,64,128]{2,1,0:T(8,128)S(1)}, f32[16,64,128]{2,1,0:T(8,128)}, u32[]{:S(2)}) copy-start(f32[16,64,128]{2,1,0:T(8,128)} %refs_2_.1) | copy-start | bytes 1572868
  0.0 10.4 %copy-start.1 = (f32[8,32,64]{2,1,0:T(8,128)S(1)}, f32[8,32,64]{2,1,0:T(8,128)}, u32[]{:S(2)}) copy-start(f32[8,32,64]{2,1,0:T(8,128)} %coarse.1) | copy-start | bytes 196612
  2.5 7.9 %collective-permute-start = (f32[3,64,128]{2,1,0:T(8,128)S(1)}, f32[3,64,128]{2,1,0:T(8,128)S(1)}, u32[]{:S(2)}, u32[]{:S(2)}) collective-permute-start(f32[3,64,128]{2,1,0:T(8,128)S(1)} %get-tuple-element.43), channel_id=1, source_target_pairs={{0,1},{1,0},{2,3},{3,2},{4,5},{5,4},{6,7},{7,6},{8,9},{9,8},{10,11... | collective-permute-start | bytes 294920 | tf_op jit(solution)/shard_map/ppermute | solution.py:59
  3.1 7.4 %collective-permute-start.2 = (f32[64,128]{1,0:T(8,128)S(1)}, f32[64,128]{1,0:T(8,128)S(1)}, u32[]{:S(2)}, u32[]{:S(2)}) collective-permute-start(f32[64,128]{1,0:T(8,128)S(1)} %get-tuple-element.45), channel_id=1, source_target_pairs={{0,2},{2,4},{4,6},{6,0},{1,3},{3,5},{5,7},{7,1},{8,10},{10,12},{12... | collective-permute-start | bytes 98312 | tf_op jit(solution)/shard_map/ppermute | solution.py:59
  5.7 4.7 %collective-permute-start.1 = (f32[48,128]{1,0:T(8,128)S(1)}, f32[48,128]{1,0:T(8,128)S(1)}, u32[]{:S(2)}, u32[]{:S(2)}) collective-permute-start(f32[48,128]{1,0:T(8,128)S(1)} %get-tuple-element.44), channel_id=1, source_target_pairs={{0,8},{8,16},{16,24},{24,0},{1,9},{9,17},{17,25},{25,1},{2,10},{10... | collective-permute-start | bytes 73736 | tf_op jit(solution)/shard_map/ppermute | solution.py:59
  11.0 1.6 %collective-permute-start.3 = (f32[424,128]{1,0:T(8,128)S(1)}, f32[424,128]{1,0:T(8,128)S(1)}, u32[]{:S(2)}, u32[]{:S(2)}) collective-permute-start(f32[424,128]{1,0:T(8,128)S(1)} %get-tuple-element.46), channel_id=1, source_target_pairs={{0,1},{1,0},{2,3},{3,2},{4,5},{5,4},{6,7},{7,6},{8,9},{9,8},{10,11... | collective-permute-start | bytes 651272 | tf_op jit(solution)/shard_map/ppermute | solution.py:64
  11.4 8.4 %collective-permute-start.8 = (f32[320,128]{1,0:T(8,128)S(1)}, f32[320,128]{1,0:T(8,128)S(1)}, u32[]{:S(2)}, u32[]{:S(2)}) collective-permute-start(f32[320,128]{1,0:T(8,128)S(1)} %get-tuple-element.72), channel_id=1, source_target_pairs={{0,1},{1,0},{2,3},{3,2},{4,5},{5,4},{6,7},{7,6},{8,9},{9,8},{10,11... | collective-permute-start | bytes 491528 | tf_op jit(solution)/shard_map/ppermute | solution.py:59
  12.8 5.6 %collective-permute-start.4 = (f32[56,128]{1,0:T(8,128)S(1)}, f32[56,128]{1,0:T(8,128)S(1)}, u32[]{:S(2)}, u32[]{:S(2)}) collective-permute-start(f32[56,128]{1,0:T(8,128)S(1)} %get-tuple-element.55), channel_id=1, source_target_pairs={{0,8},{8,0},{16,24},{24,16},{1,9},{9,1},{17,25},{25,17},{2,10},{10... | collective-permute-start | bytes 86024 | tf_op jit(solution)/shard_map/ppermute | solution.py:64
  13.7 4.7 %collective-permute-start.5 = (f32[56,128]{1,0:T(8,128)S(1)}, f32[56,128]{1,0:T(8,128)S(1)}, u32[]{:S(2)}, u32[]{:S(2)}) collective-permute-start(f32[56,128]{1,0:T(8,128)S(1)} %get-tuple-element.56), channel_id=1, source_target_pairs={{0,1},{1,0},{8,16},{9,17},{16,8},{17,9},{24,25},{25,24},{2,3},{3,2... | collective-permute-start | bytes 86024 | tf_op jit(solution)/shard_map/ppermute | solution.py:81
  13.8 6.0 %collective-permute-start.9 = (f32[80,128]{1,0:T(8,128)S(1)}, f32[80,128]{1,0:T(8,128)S(1)}, u32[]{:S(2)}, u32[]{:S(2)}) collective-permute-start(f32[80,128]{1,0:T(8,128)S(1)} %shard_map.52.refs_8_), channel_id=1, source_target_pairs={{0,24},{8,0},{16,8},{24,16},{1,25},{9,1},{17,9},{25,17},{2,26},{10... | collective-permute-start | bytes 122888 | tf_op jit(solution)/shard_map/ppermute | solution.py:59
  15.9 3.9 %collective-permute-start.10 = (f32[64,128]{1,0:T(8,128)S(1)}, f32[64,128]{1,0:T(8,128)S(1)}, u32[]{:S(2)}, u32[]{:S(2)}) collective-permute-start(f32[64,128]{1,0:T(8,128)S(1)} %get-tuple-element.73), channel_id=1, source_target_pairs={{0,6},{2,0},{4,2},{6,4},{1,7},{3,1},{5,3},{7,5},{8,14},{10,8},{12,... | collective-permute-start | bytes 98312 | tf_op jit(solution)/shard_map/ppermute | solution.py:59
  19.1 3.9 %collective-permute-start.6 = (f32[56,128]{1,0:T(8,128)S(1)}, f32[56,128]{1,0:T(8,128)S(1)}, u32[]{:S(2)}, u32[]{:S(2)}) collective-permute-start(f32[56,128]{1,0:T(8,128)S(1)} %get-tuple-element.66), channel_id=1, source_target_pairs={{0,2},{2,0},{4,6},{6,4},{1,3},{3,1},{5,7},{7,5},{8,10},{10,8},{12,... | collective-permute-start | bytes 86024 | tf_op jit(solution)/shard_map/ppermute | solution.py:64
  19.2 3.9 %collective-permute-start.7 = (f32[56,128]{1,0:T(8,128)S(1)}, f32[56,128]{1,0:T(8,128)S(1)}, u32[]{:S(2)}, u32[]{:S(2)}) collective-permute-start(f32[56,128]{1,0:T(8,128)S(1)} %get-tuple-element.67), channel_id=1, source_target_pairs={{0,1},{1,0},{2,4},{3,5},{4,2},{5,3},{6,7},{7,6},{8,9},{9,8},{10,12... | collective-permute-start | bytes 86024 | tf_op jit(solution)/shard_map/ppermute | solution.py:81
where the time goes:
time: 37.3 us; the launch traced here: 37.2 us
  blocking collectives  11.4 us (31%)
  starting transfers between devices  10.7 us (29%)
  Pallas kernels  9.58 us (26%)
  waiting for transfers between devices  5.32 us (14%)
    all_to_all x1, blocking collectives, local(): sums = lax.all_to_all(sums, ('gx', 'gy', 'gz'), 0, 0)  11.4 us
    ppermute x6, starting transfers between devices, ring(): lax.ppermute(value, axis, [(i, (i + step) % size) for i in range(size)])  9.58 us
    pallas_call x11, Pallas kernels, apply(): run(*(pltpu.with_memory_space_constraint(a, space) for a, space in zip(ar...  9.58 us
    ppermute x6, waiting for transfers between devices, ring(): lax.ppermute(value, axis, [(i, (i + step) % size) for i in range(size)])  3.78 us
    ppermute x3, waiting for transfers between devices, swap(): out = [lax.ppermute(values[0], axis, [(i, i ^ 1) for i in range(size)])]  1.54 us
    ppermute x3, starting transfers between devices, swap(): out = [lax.ppermute(values[0], axis, [(i, i ^ 1) for i in range(size)])]  1.09 us
  transfers between devices with their start and end apart: 11, of which 3 were waited for; matrix products, arithmetic and copies ran while one was open for 0% of the time, Pallas kernels for 10%

commit v1 on v0

--- a/solution.py
+++ b/solution.py
@@ -165,8 +165,8 @@
                 spot = k * nz + z
                 up_x[spot : spot + 1, :] = s[k][nx - 1 :, :]
                 low_x[spot : spot + 1, :] = s[k][:1, :]
-                high = jnp.where(lane == spot, shift_lanes(s[k], spot + 1), high)
-                low = jnp.where(lane == spot, shift_lanes(s[k], spot), low)
+                high = jnp.where(lane == 2 * spot + 1, shift_lanes(s[k], 2 * spot + 2), high)
+                low = jnp.where(lane == 2 * spot, shift_lanes(s[k], 2 * spot), low)
                 if z == 0:
                     low_z[k] = s[k]
                 if z == nz - 1:
@@ -227,7 +227,7 @@
                 if z == 0:
                     total += below_z
                 total += jnp.where(row == 0, from_below("gx", gx[nz + z : nz + z + 1, :]), 0.0)
-                total += jnp.where(lane == 0, shift_lanes(below_y, -(2 * nz + z)), 0.0)
+                total += jnp.where(lane == 0, shift_lanes(below_y, -(4 * nz + 2 * z + 1)), 0.0)
                 guess = total / (6.0 + shift[z])
                 fg[z] = guess
                 both.append(guess)
@@ -450,7 +450,7 @@
         got = refs[:gots]
         rhs, w, up_, down_, part, inv, _, rhs3, w3 = refs[gots : gots + 9]
         rest = refs[gots + 9 :]
-        out, (add,) = rest[:sends], rest[sends:]
+        out = rest
         lane_p = lane_ids(planes)
 
         def take_at(pick, at):
@@ -460,9 +460,9 @@
         def take(pick, i):
             return take_at(pick, slice(i * planes, (i + 1) * planes))
 
-        add[...] = jnp.zeros_like(add)
         for c in range(planes):
             w3[c] = w[c]
+            rhs3[c] = rhs[c]
         for pick, near, far, edge in ((high_of, cx, cx + 1, cx - 1), (low_of, rows - 1, rows - 2, 0)):
             first, second, third = take(pick, 0), take(pick, 1), take(pick, 2)
             other = shift_lanes(third, -cy)
@@ -473,12 +473,10 @@
                 value = jnp.where(lane_p < cy, value, 0.0)
                 value += jnp.where(lane_p == cy, shift_lanes(ends, 1), 0.0)
                 value += jnp.where(lane_p == LANES - 1, shift_lanes(ends, -1), 0.0)
-                add[:, at, :] = value
+                rhs3[:, at, :] += value
             w3[:, near, :] = jnp.where(lane_p < cy, second, 0.0)
             w3[:, far, :] = jnp.where(lane_p < cy, shift_lanes(second, -cy), 0.0)
-            add[:, edge, :] = jnp.where(lane_p < cy, third, 0.0)
-        for c in range(planes):
-            rhs3[c] = rhs[c] + add[c]
+            rhs3[:, edge, :] += jnp.where(lane_p < cy, third, 0.0)
 
         lane_c = lane_ids(rows)
         lane8 = lane_ids(8)
@@ -527,7 +525,6 @@
     return call(
         body,
         [whole, whole] + [(cut + half, LANES)] * sends,
-        scratch=[whole],
         in_specs=vmem(gots + 7),
         out_specs=vmem(2 + sends),
     )(*got, rhs, w, *early)
@@ -672,9 +669,8 @@
         tz, gx, ty, _, out = refs[5:]
         lane = lane_ids(nx)
         row = row_ids(nx)
-        y_low = from_below("gy", ly[...])
-
-        y_high = from_above("gy", counts[2], ty[...])
+
+        ends = from_below("gy", ly[...]) + from_above("gy", counts[2], ty[...])
         for k in range(3):
             z_low = from_below("gz", lz[k])
             z_high = from_above("gz", counts[0], tz[k * nx : (k + 1) * nx, :])
@@ -687,9 +683,9 @@
                 around += jnp.where(row == 0, x_low[z : z + 1, :], shift_rows(here, 1))
                 around += jnp.where(row == nx - 1, x_high[z : z + 1, :], shift_rows(here, -1))
                 spot = k * nz + z
-                around += jnp.where(lane == 0, shift_lanes(y_low, -spot), shift_lanes(here, 1))
-                right = shift_lanes(y_high, -spot - 1)
-                around += jnp.where(lane == LANES - 1, right, shift_lanes(here, -1))
+                end = shift_lanes(ends, LANES - 1 - 2 * spot)
+                around += jnp.where(lane == 0, end, shift_lanes(here, 1))
+                around += jnp.where(lane == LANES - 1, end, shift_lanes(here, -1))
                 out[k, z] = here + around * inv[k, z]
 
     return call(
@@ -796,14 +792,19 @@
         x_value = from_above("gx", counts[1], x_value)
 
         lane_c = lane_ids(rows)
-        even = jnp.zeros((rows, LANES), F32)
-        odd = jnp.zeros((rows, LANES), F32)
+        middle = jnp.zeros((rows, LANES), F32)
+        inward = jnp.zeros((rows, LANES), F32)
+        beside = jnp.zeros((rows, LANES), F32)
         for z in range(nz):
             c = z // 2
             here = sol[c]
-            same = 3.0 * here + shift_lanes(here, 1) + sol[(c + 1 if z % 2 else c - 1) % planes]
-            even = jnp.where(lane_c == z, shift_lanes(same + shift_rows(here, 1), z - cy), even)
-            odd = jnp.where(lane_c == z, shift_lanes(same + shift_rows(here, -1), z - cy), odd)
+            same = 3.0 * here + sol[(c + 1 if z % 2 else c - 1) % planes]
+            middle = jnp.where(lane_c == z, shift_lanes(same, z - cy), middle)
+            inward = jnp.where(lane_c == z, shift_lanes(here, z - cy + 1), inward)
+            beside = jnp.where(lane_c == z, shift_lanes(here, z - cy), beside)
+        middle += inward
+        even = middle + shift_rows(beside, 1)
+        odd = middle + shift_rows(beside, -1)
         inter[0, pl.ds(0, cx, 2), :] = even[:cx, :]
         inter[0, pl.ds(1, cx, 2), :] = odd[:cx, :]
         y_base = jnp.concatenate(

time: 37.3 us -> 37 us (level)
  Pallas kernels: 9.58 us -> 9.1 us
  waiting for transfers between devices: 5.32 us -> 5.73 us
    pallas_call x11, Pallas kernels: 9.58 us -> 9.1 us  [apply(): run(*(pltpu.with_memory_space_constraint(a, space) for a, space in zip(ar...]
    ppermute x3, waiting for transfers between devices: 1.54 us -> 1.93 us  [swap(): out = [lax.ppermute(values[0], axis, [(i, i ^ 1) for i in range(size)])]]
  transfers between devices with their start and end apart: 11 -> 11, of which waited for: 3 -> 3; matrix products, arithmetic and copies ran while one was open for 0% -> 0% of each run, Pallas kernels for 10% -> 9%
where the time goes in v1:
time: 37 us; the launch traced here: 36.9 us
  blocking collectives  11.2 us (30%)
  starting transfers between devices  10.7 us (29%)
  Pallas kernels  9.1 us (25%)
  waiting for transfers between devices  5.73 us (15%)
    all_to_all x1, blocking collectives, local(): sums = lax.all_to_all(sums, ('gx', 'gy', 'gz'), 0, 0)  11.2 us
    ppermute x6, starting transfers between devices, ring(): lax.ppermute(value, axis, [(i, (i + step) % size) for i in range(size)])  9.58 us
    pallas_call x11, Pallas kernels, apply(): run(*(pltpu.with_memory_space_constraint(a, space) for a, space in zip(ar...  9.1 us
    ppermute x6, waiting for transfers between devices, ring(): lax.ppermute(value, axis, [(i, (i + step) % size) for i in range(size)])  3.79 us
    ppermute x3, waiting for transfers between devices, swap(): out = [lax.ppermute(values[0], axis, [(i, i ^ 1) for i in range(size)])]  1.93 us
    ppermute x3, starting transfers between devices, swap(): out = [lax.ppermute(values[0], axis, [(i, i ^ 1) for i in range(size)])]  1.09 us
  transfers between devices with their start and end apart: 11, of which 3 were waited for; matrix products, arithmetic and copies ran while one was open for 0% of the time, Pallas kernels for 9%

profile of v1, /device:TPU:0, one launch (start us, length us, event | category | flops | bytes accessed | tf_op | source)
XLA Modules:
  0.0 36.9 jit_solution(17680588759754950580)
XLA Ops:
  0.0 2.5 %shard_map.46 = (f32[16,64,128]{2,1,0:T(8,128)S(1)}, f32[3,64,128]{2,1,0:T(8,128)S(1)}, f32[48,128]{1,0:T(8,128)S(1)}, f32[64,128]{1,0:T(8,128)S(1)}, f32[3,64,1...) custom-call(f32[3,16,64,128]{3,2,1,0:T(8,128)} %res.1, ...), custom_call_target="tpu_custom_call" | custom-call | tf_op jit(solution)/shard_map/pallas_call | solution.py:113
  2.5 0.6 %collective-permute-start = (f32[3,64,128]{2,1,0:T(8,128)S(1)}, f32[3,64,128]{2,1,0:T(8,128)S(1)}, u32[]{:S(2)}, u32[]{:S(2)}) collective-permute-start(f32[3,64,128]{2,1,0:T(8,128)S(1)} %get-tuple-element.43), channel_id=1, source_target_pairs={{0,1},{1,0},{2,3},{3,2},{4,5},{5,4},{6,7},{7,6},{8,9},{9,8},{10,11... | collective-permute-start | bytes 294920 | tf_op jit(solution)/shard_map/ppermute | solution.py:59
  3.1 2.6 %collective-permute-start.2 = (f32[64,128]{1,0:T(8,128)S(1)}, f32[64,128]{1,0:T(8,128)S(1)}, u32[]{:S(2)}, u32[]{:S(2)}) collective-permute-start(f32[64,128]{1,0:T(8,128)S(1)} %get-tuple-element.45), channel_id=1, source_target_pairs={{0,2},{2,4},{4,6},{6,0},{1,3},{3,5},{5,7},{7,1},{8,10},{10,12},{12... | collective-permute-start | bytes 98312 | tf_op jit(solution)/shard_map/ppermute | solution.py:59
  5.7 1.5 %collective-permute-start.1 = (f32[48,128]{1,0:T(8,128)S(1)}, f32[48,128]{1,0:T(8,128)S(1)}, u32[]{:S(2)}, u32[]{:S(2)}) collective-permute-start(f32[48,128]{1,0:T(8,128)S(1)} %get-tuple-element.44), channel_id=1, source_target_pairs={{0,8},{8,16},{16,24},{24,0},{1,9},{9,17},{17,25},{25,1},{2,10},{10... | collective-permute-start | bytes 73736 | tf_op jit(solution)/shard_map/ppermute | solution.py:59
  7.2 3.2 %collective-permute-done.1.gx.refs_3_ = f32[48,128]{1,0:T(8,128)S(1)} collective-permute-done((f32[48,128]{1,0:T(8,128)S(1)}, f32[48,128]{1,0:T(8,128)S(1)}, u32[]{:S(2)}, u32[]{:S(2)}) %collective-permute-start.1) | collective-permute-done | bytes 24608 | tf_op jit(solution)/shard_map/ppermute | solution.py:59
  10.4 0.5 %shard_map.47 = (f32[16,64,128]{2,1,0:T(8,128)S(1)}, f32[12,40,128]{2,1,0:T(8,128)S(1)}, f32[8,40,128]{2,1,0:T(8,128)S(1)}, f32[8,40,128]{2,1,0:T(8,128)S(1)}, f...) custom-call(f32[16,64,128]{2,1,0:T(8,128)S(1)} %get-tuple-element.42.part, f32[16,64,128]{2,1,0:T(8,128)S(1)} %copy-done, ...), custom_call_target="tpu_custom_call" | custom-call | tf_op jit(solution)/shard_map/pallas_call | solution.py:113
  11.0 0.1 collective-permute-start.3
  11.1 0.4 shard_map.48
  11.4 0.6 %collective-permute-start.8 = (f32[320,128]{1,0:T(8,128)S(1)}, f32[320,128]{1,0:T(8,128)S(1)}, u32[]{:S(2)}, u32[]{:S(2)}) collective-permute-start(f32[320,128]{1,0:T(8,128)S(1)} %get-tuple-element.72), channel_id=1, source_target_pairs={{0,1},{1,0},{2,3},{3,2},{4,5},{5,4},{6,7},{7,6},{8,9},{9,8},{10,11... | collective-permute-start | bytes 491528 | tf_op jit(solution)/shard_map/ppermute | solution.py:59
  12.0 0.6 %shard_map.49 = (f32[64,128]{1,0:T(8,128)S(1)}, f32[64,128]{1,0:T(8,128)S(1)}, f32[64,128]{1,0:T(8,128)S(1)}, f32[64,128]{1,0:T(8,128)S(1)}) custom-call(f32[16,64,128]{2,1,0:T(8,128)S(1)} %get-tuple-element.51.fg.refs_5_.refs_1_.refs_3_, f32[16,64,128]{2,1,0:T(8,128)S(1)} %copy-done), custom_call_target="tpu_custom_call" | custom-call | tf_op jit(solution)/shard_map/pallas_call | solution.py:113
  12.6 0.2 shard_map.50
  12.8 1.0 %collective-permute-start.4 = (f32[56,128]{1,0:T(8,128)S(1)}, f32[56,128]{1,0:T(8,128)S(1)}, u32[]{:S(2)}, u32[]{:S(2)}) collective-permute-start(f32[56,128]{1,0:T(8,128)S(1)} %get-tuple-element.55), channel_id=1, source_target_pairs={{0,8},{8,0},{16,24},{24,16},{1,9},{9,1},{17,25},{25,17},{2,10},{10... | collective-permute-start | bytes 86024 | tf_op jit(solution)/shard_map/ppermute | solution.py:64
  13.7 0.1 shard_map.52.refs_8_
  13.8 2.1 %collective-permute-start.9 = (f32[80,128]{1,0:T(8,128)S(1)}, f32[80,128]{1,0:T(8,128)S(1)}, u32[]{:S(2)}, u32[]{:S(2)}) collective-permute-start(f32[80,128]{1,0:T(8,128)S(1)} %shard_map.52.refs_8_), channel_id=1, source_target_pairs={{0,24},{8,0},{16,8},{24,16},{1,25},{9,1},{17,9},{25,17},{2,26},{10... | collective-permute-start | bytes 122888 | tf_op jit(solution)/shard_map/ppermute | solution.py:59
  15.9 2.2 %collective-permute-start.10 = (f32[64,128]{1,0:T(8,128)S(1)}, f32[64,128]{1,0:T(8,128)S(1)}, u32[]{:S(2)}, u32[]{:S(2)}) collective-permute-start(f32[64,128]{1,0:T(8,128)S(1)} %get-tuple-element.73), channel_id=1, source_target_pairs={{0,6},{2,0},{4,2},{6,4},{1,7},{3,1},{5,3},{7,5},{8,14},{10,8},{12,... | collective-permute-start | bytes 98312 | tf_op jit(solution)/shard_map/ppermute | solution.py:59
  18.2 0.2 shard_map.51
  18.4 0.7 %shard_map.53 = (f32[12,40,128]{2,1,0:T(8,128)S(1)}, f32[12,40,128]{2,1,0:T(8,128)S(1)}, f32[56,128]{1,0:T(8,128)S(1)}, f32[56,128]{1,0:T(8,128)S(1)}) custom-call(f32[56,128]{1,0:T(8,128)S(1)} %collective-permute-done.4.refs_0_.refs_11_, f32[56,128]{1,0:T(8,128)S(1)} %collective-permute-done.5.refs_1_.refs_12_, ...), custom_call_target="tpu_custom_call" | custom-call | tf_op jit(solution)/shard_map/pallas_call | solution.py:113
  19.2 0.1 collective-permute-start.7
  19.3 0.5 %collective-permute-done.10.refs_7_ = f32[64,128]{1,0:T(8,128)S(1)} collective-permute-done((f32[64,128]{1,0:T(8,128)S(1)}, f32[64,128]{1,0:T(8,128)S(1)}, u32[]{:S(2)}, u32[]{:S(2)}) %collective-permute-start.10) | collective-permute-done | bytes 32800 | tf_op jit(solution)/shard_map/ppermute | solution.py:59
  19.8 1.3 %shard_map.54.refs_4_.refs_6_ = f32[3,16,64,128]{3,2,1,0:T(8,128)S(1)} custom-call(f32[3,16,64,128]{3,2,1,0:T(8,128)S(1)} %get-tuple-element.70.refs_0_, f32[3,16,64,128]{3,2,1,0:T(8,128)S(1)} %get-tuple-element.71.refs_1_, f32[3,64,128]{2,1,0:T(8,128)S(1)} %collective-permute-done.gz.refs_2_, f32[48,128]{1,0:T(8,128)S(1)} %collective-permute-done.1.gx.refs_3_, ...), custom_call_target="tpu_custom_call" | custom-call | tf_op jit(solution)/shard_map/pallas_call | solution.py:113
  21.1 1.9 %collective-permute-done.6.refs_0_.refs_13_ = f32[56,128]{1,0:T(8,128)S(1)} collective-permute-done((f32[56,128]{1,0:T(8,128)S(1)}, f32[56,128]{1,0:T(8,128)S(1)}, u32[]{:S(2)}, u32[]{:S(2)}) %collective-permute-start.6) | collective-permute-done | bytes 28704 | tf_op jit(solution)/shard_map/ppermute | solution.py:64
  23.1 0.7 %shard_map.55 = (f32[12,40,128]{2,1,0:T(8,128)S(1)}, f32[12,40,128]{2,1,0:T(8,128)S(1)}, f32[32,1,128]{2,1,0:T(1,128)S(1)}) custom-call(f32[56,128]{1,0:T(8,128)S(1)} %collective-permute-done.6.refs_0_.refs_13_, f32[56,128]{1,0:T(8,128)S(1)} %collective-permute-done.7.refs_1_.refs_14_, f32[12,40,128]{2,1,0:T(8,128)S(1)} %get-tuple-element.68.refs_2_, ...), custom_call_target="tpu_custom_call" | custom-call | tf_op jit(solution)/shard_map/pallas_call | solution.py:113
  23.7 11.2 %all_to_all.5.refs_0_ = f32[32,1,128]{2,1,0:T(1,128)S(1)} all-to-all(f32[32,1,128]{2,1,0:T(1,128)S(1)} %get-tuple-element.74), channel_id=1, replica_groups=mesh['gx'=4,'gy'=4,'gz'=2] {'gx','gy','gz'}, dimensions={0} | all-to-all | bytes 32768 | tf_op jit(solution)/shard_map/all_to_all | solution.py:882
  34.9 2.0 %shard_map.56 = f32[3,16,64,128]{3,2,1,0:T(8,128)} custom-call(f32[32,1,128]{2,1,0:T(1,128)S(1)} %all_to_all.5.refs_0_, f32[12,40,128]{2,1,0:T(8,128)S(1)} %get-tuple-element.75.refs_1_, f32[12,40,128]{2,1,0:T(8,128)S(1)} %get-tuple-element.76.refs_2_, f32[16,64,128]{2,1,0:T(8,128)S(1)} %get-tuple-element.51.fg.refs_5_.refs_1_.refs_3_, ...), custom_call_target="tpu_custom_call" | custom-call | tf_op jit(solution)/shard_map/pallas_call | solution.py:113
  (14 shorter events, 0.1 us)
Async XLA Ops:
  0.0 10.4 %copy-start = (f32[16,64,128]{2,1,0:T(8,128)S(1)}, f32[16,64,128]{2,1,0:T(8,128)}, u32[]{:S(2)}) copy-start(f32[16,64,128]{2,1,0:T(8,128)} %refs_2_.1) | copy-start | bytes 1572868
  0.0 10.4 %copy-start.1 = (f32[8,32,64]{2,1,0:T(8,128)S(1)}, f32[8,32,64]{2,1,0:T(8,128)}, u32[]{:S(2)}) copy-start(f32[8,32,64]{2,1,0:T(8,128)} %coarse.1) | copy-start | bytes 196612
  2.5 7.9 %collective-permute-start = (f32[3,64,128]{2,1,0:T(8,128)S(1)}, f32[3,64,128]{2,1,0:T(8,128)S(1)}, u32[]{:S(2)}, u32[]{:S(2)}) collective-permute-start(f32[3,64,128]{2,1,0:T(8,128)S(1)} %get-tuple-element.43), channel_id=1, source_target_pairs={{0,1},{1,0},{2,3},{3,2},{4,5},{5,4},{6,7},{7,6},{8,9},{9,8},{10,11... | collective-permute-start | bytes 294920 | tf_op jit(solution)/shard_map/ppermute | solution.py:59
  3.1 7.4 %collective-permute-start.2 = (f32[64,128]{1,0:T(8,128)S(1)}, f32[64,128]{1,0:T(8,128)S(1)}, u32[]{:S(2)}, u32[]{:S(2)}) collective-permute-start(f32[64,128]{1,0:T(8,128)S(1)} %get-tuple-element.45), channel_id=1, source_target_pairs={{0,2},{2,4},{4,6},{6,0},{1,3},{3,5},{5,7},{7,1},{8,10},{10,12},{12... | collective-permute-start | bytes 98312 | tf_op jit(solution)/shard_map/ppermute | solution.py:59
  5.7 4.7 %collective-permute-start.1 = (f32[48,128]{1,0:T(8,128)S(1)}, f32[48,128]{1,0:T(8,128)S(1)}, u32[]{:S(2)}, u32[]{:S(2)}) collective-permute-start(f32[48,128]{1,0:T(8,128)S(1)} %get-tuple-element.44), channel_id=1, source_target_pairs={{0,8},{8,16},{16,24},{24,0},{1,9},{9,17},{17,25},{25,1},{2,10},{10... | collective-permute-start | bytes 73736 | tf_op jit(solution)/shard_map/ppermute | solution.py:59
  11.0 1.6 %collective-permute-start.3 = (f32[424,128]{1,0:T(8,128)S(1)}, f32[424,128]{1,0:T(8,128)S(1)}, u32[]{:S(2)}, u32[]{:S(2)}) collective-permute-start(f32[424,128]{1,0:T(8,128)S(1)} %get-tuple-element.46), channel_id=1, source_target_pairs={{0,1},{1,0},{2,3},{3,2},{4,5},{5,4},{6,7},{7,6},{8,9},{9,8},{10,11... | collective-permute-start | bytes 651272 | tf_op jit(solution)/shard_map/ppermute | solution.py:64
  11.4 8.4 %collective-permute-start.8 = (f32[320,128]{1,0:T(8,128)S(1)}, f32[320,128]{1,0:T(8,128)S(1)}, u32[]{:S(2)}, u32[]{:S(2)}) collective-permute-start(f32[320,128]{1,0:T(8,128)S(1)} %get-tuple-element.72), channel_id=1, source_target_pairs={{0,1},{1,0},{2,3},{3,2},{4,5},{5,4},{6,7},{7,6},{8,9},{9,8},{10,11... | collective-permute-start | bytes 491528 | tf_op jit(solution)/shard_map/ppermute | solution.py:59
  12.8 5.6 %collective-permute-start.4 = (f32[56,128]{1,0:T(8,128)S(1)}, f32[56,128]{1,0:T(8,128)S(1)}, u32[]{:S(2)}, u32[]{:S(2)}) collective-permute-start(f32[56,128]{1,0:T(8,128)S(1)} %get-tuple-element.55), channel_id=1, source_target_pairs={{0,8},{8,0},{16,24},{24,16},{1,9},{9,1},{17,25},{25,17},{2,10},{10... | collective-permute-start | bytes 86024 | tf_op jit(solution)/shard_map/ppermute | solution.py:64
  13.7 4.7 %collective-permute-start.5 = (f32[56,128]{1,0:T(8,128)S(1)}, f32[56,128]{1,0:T(8,128)S(1)}, u32[]{:S(2)}, u32[]{:S(2)}) collective-permute-start(f32[56,128]{1,0:T(8,128)S(1)} %get-tuple-element.56), channel_id=1, source_target_pairs={{0,1},{1,0},{8,16},{9,17},{16,8},{17,9},{24,25},{25,24},{2,3},{3,2... | collective-permute-start | bytes 86024 | tf_op jit(solution)/shard_map/ppermute | solution.py:81
  13.8 6.0 %collective-permute-start.9 = (f32[80,128]{1,0:T(8,128)S(1)}, f32[80,128]{1,0:T(8,128)S(1)}, u32[]{:S(2)}, u32[]{:S(2)}) collective-permute-start(f32[80,128]{1,0:T(8,128)S(1)} %shard_map.52.refs_8_), channel_id=1, source_target_pairs={{0,24},{8,0},{16,8},{24,16},{1,25},{9,1},{17,9},{25,17},{2,26},{10... | collective-permute-start | bytes 122888 | tf_op jit(solution)/shard_map/ppermute | solution.py:59
  15.9 3.9 %collective-permute-start.10 = (f32[64,128]{1,0:T(8,128)S(1)}, f32[64,128]{1,0:T(8,128)S(1)}, u32[]{:S(2)}, u32[]{:S(2)}) collective-permute-start(f32[64,128]{1,0:T(8,128)S(1)} %get-tuple-element.73), channel_id=1, source_target_pairs={{0,6},{2,0},{4,2},{6,4},{1,7},{3,1},{5,3},{7,5},{8,14},{10,8},{12,... | collective-permute-start | bytes 98312 | tf_op jit(solution)/shard_map/ppermute | solution.py:59
  19.1 3.9 %collective-permute-start.6 = (f32[56,128]{1,0:T(8,128)S(1)}, f32[56,128]{1,0:T(8,128)S(1)}, u32[]{:S(2)}, u32[]{:S(2)}) collective-permute-start(f32[56,128]{1,0:T(8,128)S(1)} %get-tuple-element.66), channel_id=1, source_target_pairs={{0,2},{2,0},{4,6},{6,4},{1,3},{3,1},{5,7},{7,5},{8,10},{10,8},{12,... | collective-permute-start | bytes 86024 | tf_op jit(solution)/shard_map/ppermute | solution.py:64
  19.2 3.9 %collective-permute-start.7 = (f32[56,128]{1,0:T(8,128)S(1)}, f32[56,128]{1,0:T(8,128)S(1)}, u32[]{:S(2)}, u32[]{:S(2)}) collective-permute-start(f32[56,128]{1,0:T(8,128)S(1)} %get-tuple-element.67), channel_id=1, source_target_pairs={{0,1},{1,0},{2,4},{3,5},{4,2},{5,3},{6,7},{7,6},{8,9},{9,8},{10,12... | collective-permute-start | bytes 86024 | tf_op jit(solution)/shard_map/ppermute | solution.py:81

commit v2 on v1

--- a/solution.py
+++ b/solution.py
@@ -213,6 +213,7 @@
         lane_c = lane_ids(rows)
         row_c = row_ids(rows)
         below_z = from_below("gz", gz[0])
+        below_x = from_below("gx", gx[nz : 2 * nz, :])
         below_y = from_below("gy", gy[...])
         fine = lax.broadcasted_iota(jnp.int32, (ny, 2 * LANES), 0)
         coarse_lane = lax.broadcasted_iota(jnp.int32, (ny, 2 * LANES), 1)
@@ -226,7 +227,7 @@
                 total = part[z]
                 if z == 0:
                     total += below_z
-                total += jnp.where(row == 0, from_below("gx", gx[nz + z : nz + z + 1, :]), 0.0)
+                total += jnp.where(row == 0, below_x[z : z + 1, :], 0.0)
                 total += jnp.where(lane == 0, shift_lanes(below_y, -(4 * nz + 2 * z + 1)), 0.0)
                 guess = total / (6.0 + shift[z])
                 fg[z] = guess
@@ -430,12 +431,11 @@
     return (rows + 8) // 16 * 8
 
 
-def line(source, lane, fine, at):
-    acc = jnp.zeros(lane.shape, F32)
-    for z in range(source.shape[0]):
-        moved = jnp.broadcast_to(source[z : z + 1, :], lane.shape)
-        acc = jnp.where(lane == at + z, shift_lanes(moved, at + z - fine), acc)
-    return acc
+def line(source, fine, at):
+    count = source.shape[0]
+    spread = jnp.broadcast_to(source[:, fine : fine + 1], (count, LANES))
+    own = lane_ids(count) - at == row_ids(count)
+    return jnp.sum(jnp.where(own, spread, 0.0), axis=0, keepdims=True)
 
 
 def y_stage(got, rhs, w, early, x_count, y_count):
@@ -479,7 +479,6 @@
             rhs3[:, edge, :] += jnp.where(lane_p < cy, third, 0.0)
 
         lane_c = lane_ids(rows)
-        lane8 = lane_ids(8)
         base = 5 * planes
         x_face = slice(3 * planes, 3 * planes + nz)
         x_high = take_at(high_of, x_face)
@@ -496,7 +495,7 @@
                     acc = jnp.where(there, shift_lanes(field[z], at - source), acc)
             ref[:cut, :] = acc[:cut]
             ref[: rows - cut, :] += shift_lanes(acc[cut:], base)
-            ref[cut - 8 : cut, :] += line(x_high, lane8, fine, base)
+            ref[cut - 8 : cut, :] += line(x_high, fine, base)
             ref[cut:, :] = early
 
         def up(ref):
@@ -504,8 +503,8 @@
 
         def down(ref):
             row = row_ids(nx)
-            ends = jnp.where(row == 0, line(take_at(low_of, x_face), lane8, 0, 0)[:1, :], 0.0)
-            ends += jnp.where(row == nx - 1, line(x_high, lane8, 0, 0)[:1, :], 0.0)
+            ends = jnp.where(row == 0, line(take_at(low_of, x_face), 0, 0), 0.0)
+            ends += jnp.where(row == nx - 1, line(x_high, 0, 0), 0.0)
             inverse = inv[...]
             value = part[...] + inverse * ends
             packed = down_[...]

time: 37 us -> 37 us (level)
  no operation moved by 1% of the time
where the time goes in v2:
time: 37 us; the launch traced here: 36.8 us
  blocking collectives  11.1 us (30%)
  starting transfers between devices  10.7 us (29%)
  Pallas kernels  9.07 us (25%)
  waiting for transfers between devices  5.73 us (15%)
    all_to_all x1, blocking collectives, local(): sums = lax.all_to_all(sums, ('gx', 'gy', 'gz'), 0, 0)  11.1 us
    ppermute x6, starting transfers between devices, ring(): lax.ppermute(value, axis, [(i, (i + step) % size) for i in range(size)])  9.58 us
    pallas_call x11, Pallas kernels, apply(): run(*(pltpu.with_memory_space_constraint(a, space) for a, space in zip(ar...  9.07 us
    ppermute x6, waiting for transfers between devices, ring(): lax.ppermute(value, axis, [(i, (i + step) % size) for i in range(size)])  3.83 us
    ppermute x3, waiting for transfers between devices, swap(): out = [lax.ppermute(values[0], axis, [(i, i ^ 1) for i in range(size)])]  1.89 us
    ppermute x3, starting transfers between devices, swap(): out = [lax.ppermute(values[0], axis, [(i, i ^ 1) for i in range(size)])]  1.08 us
  transfers between devices with their start and end apart: 11, of which 3 were waited for; matrix products, arithmetic and copies ran while one was open for 0% of the time, Pallas kernels for 9%

profile of v2, /device:TPU:0, one launch (start us, length us, event | category | flops | bytes accessed | tf_op | source)
XLA Modules:
  0.0 36.8 jit_solution(14650428524719585858)
XLA Ops:
  0.0 2.5 %shard_map.46 = (f32[16,64,128]{2,1,0:T(8,128)S(1)}, f32[3,64,128]{2,1,0:T(8,128)S(1)}, f32[48,128]{1,0:T(8,128)S(1)}, f32[64,128]{1,0:T(8,128)S(1)}, f32[3,64,1...) custom-call(f32[3,16,64,128]{3,2,1,0:T(8,128)} %res.1, ...), custom_call_target="tpu_custom_call" | custom-call | tf_op jit(solution)/shard_map/pallas_call | solution.py:113
  2.5 0.6 %collective-permute-start = (f32[3,64,128]{2,1,0:T(8,128)S(1)}, f32[3,64,128]{2,1,0:T(8,128)S(1)}, u32[]{:S(2)}, u32[]{:S(2)}) collective-permute-start(f32[3,64,128]{2,1,0:T(8,128)S(1)} %get-tuple-element.43), channel_id=1, source_target_pairs={{0,1},{1,0},{2,3},{3,2},{4,5},{5,4},{6,7},{7,6},{8,9},{9,8},{10,11... | collective-permute-start | bytes 294920 | tf_op jit(solution)/shard_map/ppermute | solution.py:59
  3.1 2.6 %collective-permute-start.2 = (f32[64,128]{1,0:T(8,128)S(1)}, f32[64,128]{1,0:T(8,128)S(1)}, u32[]{:S(2)}, u32[]{:S(2)}) collective-permute-start(f32[64,128]{1,0:T(8,128)S(1)} %get-tuple-element.45), channel_id=1, source_target_pairs={{0,2},{2,4},{4,6},{6,0},{1,3},{3,5},{5,7},{7,1},{8,10},{10,12},{12... | collective-permute-start | bytes 98312 | tf_op jit(solution)/shard_map/ppermute | solution.py:59
  5.7 1.5 %collective-permute-start.1 = (f32[48,128]{1,0:T(8,128)S(1)}, f32[48,128]{1,0:T(8,128)S(1)}, u32[]{:S(2)}, u32[]{:S(2)}) collective-permute-start(f32[48,128]{1,0:T(8,128)S(1)} %get-tuple-element.44), channel_id=1, source_target_pairs={{0,8},{8,16},{16,24},{24,0},{1,9},{9,17},{17,25},{25,1},{2,10},{10... | collective-permute-start | bytes 73736 | tf_op jit(solution)/shard_map/ppermute | solution.py:59
  7.2 3.2 %collective-permute-done.1.gx.refs_3_ = f32[48,128]{1,0:T(8,128)S(1)} collective-permute-done((f32[48,128]{1,0:T(8,128)S(1)}, f32[48,128]{1,0:T(8,128)S(1)}, u32[]{:S(2)}, u32[]{:S(2)}) %collective-permute-start.1) | collective-permute-done | bytes 24608 | tf_op jit(solution)/shard_map/ppermute | solution.py:59
  10.4 0.5 %shard_map.47 = (f32[16,64,128]{2,1,0:T(8,128)S(1)}, f32[12,40,128]{2,1,0:T(8,128)S(1)}, f32[8,40,128]{2,1,0:T(8,128)S(1)}, f32[8,40,128]{2,1,0:T(8,128)S(1)}, f...) custom-call(f32[16,64,128]{2,1,0:T(8,128)S(1)} %get-tuple-element.42.part, f32[16,64,128]{2,1,0:T(8,128)S(1)} %copy-done, ...), custom_call_target="tpu_custom_call" | custom-call | tf_op jit(solution)/shard_map/pallas_call | solution.py:113
  11.0 0.1 collective-permute-start.3
  11.1 0.4 shard_map.48
  11.4 0.6 %collective-permute-start.8 = (f32[320,128]{1,0:T(8,128)S(1)}, f32[320,128]{1,0:T(8,128)S(1)}, u32[]{:S(2)}, u32[]{:S(2)}) collective-permute-start(f32[320,128]{1,0:T(8,128)S(1)} %get-tuple-element.72), channel_id=1, source_target_pairs={{0,1},{1,0},{2,3},{3,2},{4,5},{5,4},{6,7},{7,6},{8,9},{9,8},{10,11... | collective-permute-start | bytes 491528 | tf_op jit(solution)/shard_map/ppermute | solution.py:59
  12.0 0.6 %shard_map.49 = (f32[64,128]{1,0:T(8,128)S(1)}, f32[64,128]{1,0:T(8,128)S(1)}, f32[64,128]{1,0:T(8,128)S(1)}, f32[64,128]{1,0:T(8,128)S(1)}) custom-call(f32[16,64,128]{2,1,0:T(8,128)S(1)} %get-tuple-element.51.fg.refs_5_.refs_1_.refs_3_, f32[16,64,128]{2,1,0:T(8,128)S(1)} %copy-done), custom_call_target="tpu_custom_call" | custom-call | tf_op jit(solution)/shard_map/pallas_call | solution.py:113
  12.6 0.2 shard_map.50
  12.8 0.9 %collective-permute-start.4 = (f32[56,128]{1,0:T(8,128)S(1)}, f32[56,128]{1,0:T(8,128)S(1)}, u32[]{:S(2)}, u32[]{:S(2)}) collective-permute-start(f32[56,128]{1,0:T(8,128)S(1)} %get-tuple-element.55), channel_id=1, source_target_pairs={{0,8},{8,0},{16,24},{24,16},{1,9},{9,1},{17,25},{25,17},{2,10},{10... | collective-permute-start | bytes 86024 | tf_op jit(solution)/shard_map/ppermute | solution.py:64
  13.7 0.1 shard_map.52.refs_8_
  13.8 2.1 %collective-permute-start.9 = (f32[80,128]{1,0:T(8,128)S(1)}, f32[80,128]{1,0:T(8,128)S(1)}, u32[]{:S(2)}, u32[]{:S(2)}) collective-permute-start(f32[80,128]{1,0:T(8,128)S(1)} %shard_map.52.refs_8_), channel_id=1, source_target_pairs={{0,24},{8,0},{16,8},{24,16},{1,25},{9,1},{17,9},{25,17},{2,26},{10... | collective-permute-start | bytes 122888 | tf_op jit(solution)/shard_map/ppermute | solution.py:59
  15.9 2.2 %collective-permute-start.10 = (f32[64,128]{1,0:T(8,128)S(1)}, f32[64,128]{1,0:T(8,128)S(1)}, u32[]{:S(2)}, u32[]{:S(2)}) collective-permute-start(f32[64,128]{1,0:T(8,128)S(1)} %get-tuple-element.73), channel_id=1, source_target_pairs={{0,6},{2,0},{4,2},{6,4},{1,7},{3,1},{5,3},{7,5},{8,14},{10,8},{12,... | collective-permute-start | bytes 98312 | tf_op jit(solution)/shard_map/ppermute | solution.py:59
  18.2 0.2 shard_map.51
  18.4 0.7 %shard_map.53 = (f32[12,40,128]{2,1,0:T(8,128)S(1)}, f32[12,40,128]{2,1,0:T(8,128)S(1)}, f32[56,128]{1,0:T(8,128)S(1)}, f32[56,128]{1,0:T(8,128)S(1)}) custom-call(f32[56,128]{1,0:T(8,128)S(1)} %collective-permute-done.4.refs_0_.refs_11_, f32[56,128]{1,0:T(8,128)S(1)} %collective-permute-done.5.refs_1_.refs_12_, ...), custom_call_target="tpu_custom_call" | custom-call | tf_op jit(solution)/shard_map/pallas_call | solution.py:113
  19.2 0.1 collective-permute-start.7
  19.2 0.6 %collective-permute-done.10.refs_7_ = f32[64,128]{1,0:T(8,128)S(1)} collective-permute-done((f32[64,128]{1,0:T(8,128)S(1)}, f32[64,128]{1,0:T(8,128)S(1)}, u32[]{:S(2)}, u32[]{:S(2)}) %collective-permute-start.10) | collective-permute-done | bytes 32800 | tf_op jit(solution)/shard_map/ppermute | solution.py:59
  19.8 1.3 %shard_map.54.refs_4_.refs_6_ = f32[3,16,64,128]{3,2,1,0:T(8,128)S(1)} custom-call(f32[3,16,64,128]{3,2,1,0:T(8,128)S(1)} %get-tuple-element.70.refs_0_, f32[3,16,64,128]{3,2,1,0:T(8,128)S(1)} %get-tuple-element.71.refs_1_, f32[3,64,128]{2,1,0:T(8,128)S(1)} %collective-permute-done.gz.refs_2_, f32[48,128]{1,0:T(8,128)S(1)} %collective-permute-done.1.gx.refs_3_, ...), custom_call_target="tpu_custom_call" | custom-call | tf_op jit(solution)/shard_map/pallas_call | solution.py:113
  21.1 1.9 %collective-permute-done.6.refs_0_.refs_13_ = f32[56,128]{1,0:T(8,128)S(1)} collective-permute-done((f32[56,128]{1,0:T(8,128)S(1)}, f32[56,128]{1,0:T(8,128)S(1)}, u32[]{:S(2)}, u32[]{:S(2)}) %collective-permute-start.6) | collective-permute-done | bytes 28704 | tf_op jit(solution)/shard_map/ppermute | solution.py:64
  23.0 0.7 %shard_map.55 = (f32[12,40,128]{2,1,0:T(8,128)S(1)}, f32[12,40,128]{2,1,0:T(8,128)S(1)}, f32[32,1,128]{2,1,0:T(1,128)S(1)}) custom-call(f32[56,128]{1,0:T(8,128)S(1)} %collective-permute-done.6.refs_0_.refs_13_, f32[56,128]{1,0:T(8,128)S(1)} %collective-permute-done.7.refs_1_.refs_14_, f32[12,40,128]{2,1,0:T(8,128)S(1)} %get-tuple-element.68.refs_2_, ...), custom_call_target="tpu_custom_call" | custom-call | tf_op jit(solution)/shard_map/pallas_call | solution.py:113
  23.7 11.1 %all_to_all.5.refs_0_ = f32[32,1,128]{2,1,0:T(1,128)S(1)} all-to-all(f32[32,1,128]{2,1,0:T(1,128)S(1)} %get-tuple-element.74), channel_id=1, replica_groups=mesh['gx'=4,'gy'=4,'gz'=2] {'gx','gy','gz'}, dimensions={0} | all-to-all | bytes 32768 | tf_op jit(solution)/shard_map/all_to_all | solution.py:881
  34.8 2.0 %shard_map.56 = f32[3,16,64,128]{3,2,1,0:T(8,128)} custom-call(f32[32,1,128]{2,1,0:T(1,128)S(1)} %all_to_all.5.refs_0_, f32[12,40,128]{2,1,0:T(8,128)S(1)} %get-tuple-element.75.refs_1_, f32[12,40,128]{2,1,0:T(8,128)S(1)} %get-tuple-element.76.refs_2_, f32[16,64,128]{2,1,0:T(8,128)S(1)} %get-tuple-element.51.fg.refs_5_.refs_1_.refs_3_, ...), custom_call_target="tpu_custom_call" | custom-call | tf_op jit(solution)/shard_map/pallas_call | solution.py:113
  (14 shorter events, 0.1 us)
Async XLA Ops:
  0.0 10.4 %copy-start = (f32[16,64,128]{2,1,0:T(8,128)S(1)}, f32[16,64,128]{2,1,0:T(8,128)}, u32[]{:S(2)}) copy-start(f32[16,64,128]{2,1,0:T(8,128)} %refs_2_.1) | copy-start | bytes 1572868
  0.0 10.4 %copy-start.1 = (f32[8,32,64]{2,1,0:T(8,128)S(1)}, f32[8,32,64]{2,1,0:T(8,128)}, u32[]{:S(2)}) copy-start(f32[8,32,64]{2,1,0:T(8,128)} %coarse.1) | copy-start | bytes 196612
  2.5 7.9 %collective-permute-start = (f32[3,64,128]{2,1,0:T(8,128)S(1)}, f32[3,64,128]{2,1,0:T(8,128)S(1)}, u32[]{:S(2)}, u32[]{:S(2)}) collective-permute-start(f32[3,64,128]{2,1,0:T(8,128)S(1)} %get-tuple-element.43), channel_id=1, source_target_pairs={{0,1},{1,0},{2,3},{3,2},{4,5},{5,4},{6,7},{7,6},{8,9},{9,8},{10,11... | collective-permute-start | bytes 294920 | tf_op jit(solution)/shard_map/ppermute | solution.py:59
  3.1 7.4 %collective-permute-start.2 = (f32[64,128]{1,0:T(8,128)S(1)}, f32[64,128]{1,0:T(8,128)S(1)}, u32[]{:S(2)}, u32[]{:S(2)}) collective-permute-start(f32[64,128]{1,0:T(8,128)S(1)} %get-tuple-element.45), channel_id=1, source_target_pairs={{0,2},{2,4},{4,6},{6,0},{1,3},{3,5},{5,7},{7,1},{8,10},{10,12},{12... | collective-permute-start | bytes 98312 | tf_op jit(solution)/shard_map/ppermute | solution.py:59
  5.7 4.7 %collective-permute-start.1 = (f32[48,128]{1,0:T(8,128)S(1)}, f32[48,128]{1,0:T(8,128)S(1)}, u32[]{:S(2)}, u32[]{:S(2)}) collective-permute-start(f32[48,128]{1,0:T(8,128)S(1)} %get-tuple-element.44), channel_id=1, source_target_pairs={{0,8},{8,16},{16,24},{24,0},{1,9},{9,17},{17,25},{25,1},{2,10},{10... | collective-permute-start | bytes 73736 | tf_op jit(solution)/shard_map/ppermute | solution.py:59
  11.0 1.6 %collective-permute-start.3 = (f32[424,128]{1,0:T(8,128)S(1)}, f32[424,128]{1,0:T(8,128)S(1)}, u32[]{:S(2)}, u32[]{:S(2)}) collective-permute-start(f32[424,128]{1,0:T(8,128)S(1)} %get-tuple-element.46), channel_id=1, source_target_pairs={{0,1},{1,0},{2,3},{3,2},{4,5},{5,4},{6,7},{7,6},{8,9},{9,8},{10,11... | collective-permute-start | bytes 651272 | tf_op jit(solution)/shard_map/ppermute | solution.py:64
  11.4 8.4 %collective-permute-start.8 = (f32[320,128]{1,0:T(8,128)S(1)}, f32[320,128]{1,0:T(8,128)S(1)}, u32[]{:S(2)}, u32[]{:S(2)}) collective-permute-start(f32[320,128]{1,0:T(8,128)S(1)} %get-tuple-element.72), channel_id=1, source_target_pairs={{0,1},{1,0},{2,3},{3,2},{4,5},{5,4},{6,7},{7,6},{8,9},{9,8},{10,11... | collective-permute-start | bytes 491528 | tf_op jit(solution)/shard_map/ppermute | solution.py:59
  12.8 5.6 %collective-permute-start.4 = (f32[56,128]{1,0:T(8,128)S(1)}, f32[56,128]{1,0:T(8,128)S(1)}, u32[]{:S(2)}, u32[]{:S(2)}) collective-permute-start(f32[56,128]{1,0:T(8,128)S(1)} %get-tuple-element.55), channel_id=1, source_target_pairs={{0,8},{8,0},{16,24},{24,16},{1,9},{9,1},{17,25},{25,17},{2,10},{10... | collective-permute-start | bytes 86024 | tf_op jit(solution)/shard_map/ppermute | solution.py:64
  13.7 4.7 %collective-permute-start.5 = (f32[56,128]{1,0:T(8,128)S(1)}, f32[56,128]{1,0:T(8,128)S(1)}, u32[]{:S(2)}, u32[]{:S(2)}) collective-permute-start(f32[56,128]{1,0:T(8,128)S(1)} %get-tuple-element.56), channel_id=1, source_target_pairs={{0,1},{1,0},{8,16},{9,17},{16,8},{17,9},{24,25},{25,24},{2,3},{3,2... | collective-permute-start | bytes 86024 | tf_op jit(solution)/shard_map/ppermute | solution.py:81
  13.8 6.0 %collective-permute-start.9 = (f32[80,128]{1,0:T(8,128)S(1)}, f32[80,128]{1,0:T(8,128)S(1)}, u32[]{:S(2)}, u32[]{:S(2)}) collective-permute-start(f32[80,128]{1,0:T(8,128)S(1)} %shard_map.52.refs_8_), channel_id=1, source_target_pairs={{0,24},{8,0},{16,8},{24,16},{1,25},{9,1},{17,9},{25,17},{2,26},{10... | collective-permute-start | bytes 122888 | tf_op jit(solution)/shard_map/ppermute | solution.py:59
  15.9 3.9 %collective-permute-start.10 = (f32[64,128]{1,0:T(8,128)S(1)}, f32[64,128]{1,0:T(8,128)S(1)}, u32[]{:S(2)}, u32[]{:S(2)}) collective-permute-start(f32[64,128]{1,0:T(8,128)S(1)} %get-tuple-element.73), channel_id=1, source_target_pairs={{0,6},{2,0},{4,2},{6,4},{1,7},{3,1},{5,3},{7,5},{8,14},{10,8},{12,... | collective-permute-start | bytes 98312 | tf_op jit(solution)/shard_map/ppermute | solution.py:59
  19.1 3.9 %collective-permute-start.6 = (f32[56,128]{1,0:T(8,128)S(1)}, f32[56,128]{1,0:T(8,128)S(1)}, u32[]{:S(2)}, u32[]{:S(2)}) collective-permute-start(f32[56,128]{1,0:T(8,128)S(1)} %get-tuple-element.66), channel_id=1, source_target_pairs={{0,2},{2,0},{4,6},{6,4},{1,3},{3,1},{5,7},{7,5},{8,10},{10,8},{12,... | collective-permute-start | bytes 86024 | tf_op jit(solution)/shard_map/ppermute | solution.py:64
  19.2 3.9 %collective-permute-start.7 = (f32[56,128]{1,0:T(8,128)S(1)}, f32[56,128]{1,0:T(8,128)S(1)}, u32[]{:S(2)}, u32[]{:S(2)}) collective-permute-start(f32[56,128]{1,0:T(8,128)S(1)} %get-tuple-element.67), channel_id=1, source_target_pairs={{0,1},{1,0},{2,4},{3,5},{4,2},{5,3},{6,7},{7,6},{8,9},{9,8},{10,12... | collective-permute-start | bytes 86024 | tf_op jit(solution)/shard_map/ppermute | solution.py:81
